TPU v7x, 32 devices: a whole 2x2x4 slice. The times are simulated.
32 devices in a mesh: pipe: 2 (over y), dp: 4 (over z), tensor: 4 (over x, core).
Axes of the slice: x: 2, y: 2, z: 4, core: 2. Of those that a mesh axis runs over, the one named last changes fastest.
Arguments:
- saved: bfloat16 [2, 2, 256, 1024], P('pipe', None, 'dp'), may hold values from -6 to 6
- top_grad: bfloat16 [2, 256, 1024], P(None, 'dp'), may hold values from -6 to 6
- gain: bfloat16 [2, 1024], P('pipe', 'dp'), may hold values from 0.25 to 1.75
- w_query: bfloat16 [2, 1024, 1536], P('pipe', 'dp', 'tensor'), may hold values from -0.1875 to 0.1875
- w_latent: bfloat16 [2, 1024, 576], P('pipe', 'dp'), may hold values from -0.1875 to 0.1875
- compressed_gain: bfloat16 [2, 512], P('pipe', 'dp'), may hold values from 0.25 to 1.75
- expand_weight: bfloat16 [2, 512, 2048], P('pipe', 'dp', 'tensor'), may hold values from -0.25 to 0.25
- w_output: bfloat16 [2, 1024, 1024], P('pipe', 'tensor', 'dp'), may hold values from -0.1875 to 0.1875
Outputs:
- input_grad: bfloat16 [2, 2, 256, 1024], P('pipe', None, ('dp', 'tensor'))
- grad_gain: float32 [2, 1024], P('pipe', 'dp')
- grad_query: float32 [2, 1024, 1536], P('pipe', 'dp', 'tensor')
- grad_latent: float32 [2, 1024, 576], P('pipe', 'dp')
- grad_latent_gain: float32 [2, 512], P('pipe', 'dp')
- grad_expand: float32 [2, 512, 2048], P('pipe', 'dp', 'tensor')
- grad_output: float32 [2, 1024, 1024], P('pipe', 'tensor', 'dp')
All inputs are finite; a program needn't handle non-finite values.
Results may differ from a plain program's by a relative error of at most 0.04.
Values may be sent and summed in bfloat16 or wider, within the bound.
A program may use at most 64 MiB of HBM per device.

v0:
```python
import jax
import jax.numpy as jnp
from jax import lax
import numpy as np
from jax.experimental import pallas as pl
from jax.experimental.pallas import tpu as pltpu
from jax.sharding import PartitionSpec as P

NOPE = 128
ROPE = 64
VDIM = 128
COMPRESSED_RANK = 512


EPS = 1e-06


def passed_along(value, axis, steps):
    count = lax.axis_size(axis)
    first, last = (max(0, -steps), min(count, count - steps))
    return lax.ppermute(value, axis, [(source, source + steps) for source in range(first, last)])


def root_mean_scale(values, scale):
    return values * lax.rsqrt(jnp.mean(values * values, axis=-1, keepdims=True) + EPS) * scale


def rotary_angles(values):
    length = values.shape[0]
    half = values.shape[-1] // 2
    freq = jnp.exp(-jnp.log(10000.0) * jnp.arange(half, dtype=jnp.float32) / half)
    angle = jnp.arange(length, dtype=jnp.float32)[:, None] * freq[None, :]
    cosine = jnp.cos(angle)[:, None, :]
    sine = jnp.sin(angle)[:, None, :]
    first = values[..., :half]
    second = values[..., half:]
    return jnp.concatenate(
        [first * cosine - second * sine, second * cosine + first * sine], axis=-1
    )


def branch(normed, w_q, w_lat, latent_norm_gain, w_exp, w_out):
    length = normed.shape[0]
    heads = w_q.shape[1] // (NOPE + ROPE)
    rounded = normed.astype(jnp.bfloat16)
    query = jnp.dot(rounded, w_q, preferred_element_type=jnp.float32).reshape(
        length, heads, NOPE + ROPE
    )
    latent_state = jnp.dot(rounded, w_lat, preferred_element_type=jnp.float32)
    compressed_state = root_mean_scale(latent_state[:, :COMPRESSED_RANK], latent_norm_gain).astype(
        jnp.bfloat16
    )
    rotary_key_part = rotary_angles(latent_state[:, None, COMPRESSED_RANK:])[:, 0, :]
    expanded = jnp.dot(compressed_state, w_exp, preferred_element_type=jnp.float32).reshape(
        length, heads, NOPE + VDIM
    )
    key_nope = expanded[:, :, :NOPE]
    values = expanded[:, :, NOPE:].astype(jnp.bfloat16)
    query_rope = rotary_angles(query[:, :, NOPE:])
    scores = jnp.einsum("qhd,khd->hqk", query[:, :, :NOPE], key_nope) + jnp.einsum(
        "qhd,kd->hqk", query_rope, rotary_key_part
    )
    scores = scores * (NOPE + ROPE) ** (-0.5)
    causal = jnp.arange(length)[:, None] >= jnp.arange(length)[None, :]
    scores = jnp.where(causal[None], scores, -1e30)
    weights = jax.nn.softmax(scores, axis=-1).astype(jnp.bfloat16)
    mixed = jnp.einsum("hqk,khd->qhd", weights.astype(jnp.float32), values.astype(jnp.float32))
    mixed = mixed.astype(jnp.bfloat16).reshape(length, heads * VDIM)
    return jnp.dot(mixed, w_out, preferred_element_type=jnp.float32)


def shards(saved, top_grad, gain, w_query, w_latent, compressed_gain, expand_weight, w_output):
    gathered = (
        lax.all_gather(gain, "dp", axis=1, tiled=True),
        lax.all_gather(w_query, "dp", axis=1, tiled=True),
        lax.all_gather(w_latent, "dp", axis=1, tiled=True),
        lax.all_gather(compressed_gain, "dp", axis=1, tiled=True),
        lax.all_gather(expand_weight, "dp", axis=1, tiled=True),
        lax.all_gather(w_output, "dp", axis=2, tiled=True),
    )
    gain32 = gathered[0][0].astype(jnp.float32)
    query_all = gathered[1][0]
    latent_all = gathered[2][0]
    lgain32 = gathered[3][0].astype(jnp.float32)
    expand_all = gathered[4][0]
    output_all = gathered[5][0]
    sections = lax.axis_size("pipe")
    section_index = lax.axis_index("pipe")
    tensor_count = lax.axis_size("tensor")
    tensor_rank = lax.axis_index("tensor")
    micro_count = saved.shape[1]
    length = saved.shape[2]
    width = saved.shape[3]
    share = length // tensor_count

    def compute(normed, upstream):
        unused, pull = jax.vjp(
            lambda value: branch(value, query_all, latent_all, lgain32, expand_all, output_all),
            normed,
        )
        return pull(upstream.astype(jnp.float32))[0]

    def skip(normed, upstream):
        return jnp.zeros_like(normed)

    gain_total = jnp.zeros((width,), jnp.float32)
    results = jnp.zeros((micro_count, share, width), jnp.bfloat16)
    stored = jnp.zeros((micro_count, length, width), jnp.bfloat16)
    received = jnp.zeros((length, width), jnp.bfloat16)
    for tick in range(sections + micro_count - 1):
        micro = tick - (sections - 1 - section_index)
        active = jnp.logical_and(micro >= 0, micro < micro_count)
        picked = jnp.clip(micro, 0, micro_count - 1)
        x_rows = lax.dynamic_index_in_dim(saved[0], picked, 0, keepdims=False)
        top_rows = lax.dynamic_index_in_dim(top_grad, picked, 0, keepdims=False)
        arrived = received
        upstream = jnp.where(section_index == sections - 1, top_rows, arrived)
        x_float = x_rows.astype(jnp.float32)
        normed, norm_pull = jax.vjp(root_mean_scale, x_float, gain32)
        branch_grad = lax.cond(active, compute, skip, normed, upstream)
        d_normed = lax.psum(branch_grad.astype(jnp.bfloat16), "tensor").astype(jnp.float32)
        dx_norm, d_gain = norm_pull(d_normed)
        dx = (upstream.astype(jnp.float32) + dx_norm).astype(jnp.bfloat16)
        gain_total = gain_total + jnp.where(active, d_gain, 0.0)
        mine = lax.dynamic_slice_in_dim(dx, tensor_rank * share, share, 0)
        chosen = (jnp.arange(micro_count) == micro)[:, None, None]
        results = jnp.where(chosen, mine[None], results)
        stored = jnp.where(chosen, upstream[None], stored)
        received = passed_along(dx, "pipe", -1)
    totals = (
        jnp.zeros(query_all.shape, jnp.float32),
        jnp.zeros(latent_all.shape, jnp.float32),
        jnp.zeros(lgain32.shape, jnp.float32),
        jnp.zeros(expand_all.shape, jnp.float32),
        jnp.zeros(output_all.shape, jnp.float32),
    )
    for micro_index in range(micro_count):
        normed_again = root_mean_scale(saved[0, micro_index].astype(jnp.float32), gain32)
        unused, weight_pull = jax.vjp(
            lambda w_q, w_lat, lat_gain, w_exp, w_out: branch(
                normed_again, w_q, w_lat, lat_gain, w_exp, w_out
            ),
            query_all,
            latent_all,
            lgain32,
            expand_all,
            output_all,
        )
        cotangents = weight_pull(stored[micro_index].astype(jnp.float32))
        totals = tuple(
            (total + piece.astype(jnp.float32) for total, piece in zip(totals, cotangents))
        )
    gain_part = jnp.where(tensor_rank == 0, gain_total, 0.0)
    grad_q, grad_lat, grad_lg, grad_e, grad_o = totals
    out_q, part_lat, part_lg, out_e, out_o, part_gain = (
        lax.psum_scatter(grad_q.astype(jnp.bfloat16), "dp", scatter_dimension=0, tiled=True).astype(
            jnp.float32
        ),
        lax.psum_scatter(
            grad_lat.astype(jnp.bfloat16), "dp", scatter_dimension=0, tiled=True
        ).astype(jnp.float32),
        lax.psum_scatter(
            grad_lg.astype(jnp.bfloat16), "dp", scatter_dimension=0, tiled=True
        ).astype(jnp.float32),
        lax.psum_scatter(grad_e.astype(jnp.bfloat16), "dp", scatter_dimension=0, tiled=True).astype(
            jnp.float32
        ),
        lax.psum_scatter(grad_o.astype(jnp.bfloat16), "dp", scatter_dimension=1, tiled=True).astype(
            jnp.float32
        ),
        lax.psum_scatter(
            gain_part.astype(jnp.bfloat16), "dp", scatter_dimension=0, tiled=True
        ).astype(jnp.float32),
    )
    out_lat, out_lg, out_gain = (
        lax.psum(part_lat.astype(jnp.bfloat16), "tensor").astype(jnp.float32),
        lax.psum(part_lg.astype(jnp.bfloat16), "tensor").astype(jnp.float32),
        lax.psum(part_gain.astype(jnp.bfloat16), "tensor").astype(jnp.float32),
    )
    return (
        results[None],
        out_gain[None],
        out_q[None],
        out_lat[None],
        out_lg[None],
        out_e[None],
        out_o[None],
    )


MESH = pl.DeviceIdType.MESH
BF = jnp.bfloat16
F32 = jnp.float32


def mm(a, b):
    return lax.dot_general(a, b, (((1,), (0,)), ((), ())), preferred_element_type=F32)


def mm_nt(a, b):
    return lax.dot_general(a, b, (((1,), (1,)), ((), ())), preferred_element_type=F32)


def mm_tn(a, b):
    return lax.dot_general(a, b, (((0,), (0,)), ((), ())), preferred_element_type=F32)


def half_swap(v):
    lane = lax.broadcasted_iota(jnp.int32, v.shape, 1)
    ahead = pltpu.roll(v, v.shape[1] - ROPE // 2, 1)
    behind = pltpu.roll(v, ROPE // 2, 1)
    return jnp.where(lax.rem(lane, ROPE) < ROPE // 2, ahead, behind)


def section_kernel(
    dims,
    saved_ref, top_ref, gain_ref, lgain_ref, wq_ref, wl_ref, we_ref, wo_ref, cos_ref, sin_ref,
    ig_ref, gg_ref, gq_ref, gl_ref, glg_ref, ge_ref, go_ref,
    x_v, own_v, u_v, nb_v, cb_v, sm_v, wq_v, wl_v, we_v, wo_v,
    nc_v, cc_v, mx_v, uc_v, dq_v, de_v, dl_v, part_v, rs_v, lp_v, ls_v, q_v, lat_v, dx_v, sg_v, sr_v, st_v,
    own_sem, line_s, line_r, pair_s, pair_r, dp_s, dp_r, ten_s, ten_r, pipe_s, pipe_r, lat_s, lat_r,
):
    n_pipe, n, n_t, micros, seq = dims
    sec, me, ten = lax.axis_index("pipe"), lax.axis_index("dp"), lax.axis_index("tensor")
    rows = micros * seq
    chunk = seq // n_t
    share = micros * chunk
    width = x_v.shape[1]
    wcol = wq_v.shape[1]
    ccol = we_v.shape[1]
    core = lax.rem(ten, 2)
    partner = ten + 1 - 2 * core
    half = wl_ref.shape[0] // 2
    drains = []

    def rcopy(a, b, ss, rs, dev):
        return pltpu.make_async_remote_copy(
            src_ref=a, dst_ref=b, send_sem=ss, recv_sem=rs, device_id=dev, device_id_type=MESH
        )

    def begin(cond, copy):
        @pl.when(cond)
        def _():
            copy.start()

        drains.append((cond, copy))

    def dp_dev(d):
        return (sec, d, ten)

    def ten_dev(d):
        return (sec, me, d)

    barrier = pltpu.get_barrier_semaphore()
    for j in range(n):
        @pl.when(j != me)
        def _():
            pl.semaphore_signal(barrier, inc=1, device_id=dp_dev(j), device_id_type=MESH)

    for j in range(n_t):
        @pl.when(j != ten)
        def _():
            pl.semaphore_signal(barrier, inc=1, device_id=ten_dev(j), device_id_type=MESH)

        @pl.when(sec > 0)
        def _():
            pl.semaphore_signal(barrier, inc=1, device_id=(sec - 1, me, j), device_id_type=MESH)

        @pl.when(sec < n_pipe - 1)
        def _():
            pl.semaphore_signal(barrier, inc=1, device_id=(sec + 1, me, j), device_id_type=MESH)

    neighbours = jnp.minimum(sec, 1) + jnp.minimum(n_pipe - 1 - sec, 1)
    pl.semaphore_wait(barrier, n - 1 + n_t - 1 + neighbours * n_t)

    def line_start(k, source, at):
        begin(me < n - 1, rcopy(source, at(me), line_s.at[k, 0, 0], line_r.at[k, me], dp_dev(me + 1)))
        begin(me > 0, rcopy(source, at(me), line_s.at[k, 1, 0], line_r.at[k, me], dp_dev(me - 1)))

    def line_step(k, at, s, extra=None, gate=None):
        for way, block, valid, more, dest in (
            (0, jnp.maximum(me - 1 - s, 0), me - 1 - s >= 0, me < n - 1, me + 1),
            (1, jnp.minimum(me + 1 + s, n - 1), me + 1 + s <= n - 1, me > 0, me - 1),
        ):
            if gate is not None:
                valid = jnp.logical_and(valid, gate)
            arrived = rcopy(at(block), at(block), line_s.at[k, way, s + 1], line_r.at[k, block], dp_dev(dest))

            @pl.when(valid)
            def _():
                arrived.wait_recv()

            if s < n - 2:
                begin(jnp.logical_and(valid, more), arrived)
            if extra is not None:
                extra(block, valid, way, s)

    def spread_dp(k, source, dest):
        for j in range(n):
            begin(j != me, rcopy(source(j), dest.at[me], dp_s.at[k, j], dp_r.at[k, me], dp_dev(j)))

    def collect_dp(k, dest):
        for j in range(n):
            @pl.when(j != me)
            def _():
                rcopy(dest.at[j], dest.at[j], dp_s.at[k, j], dp_r.at[k, j], dp_dev(j)).wait_recv()

    def spread_ten(k, source, dest):
        for j in range(n_t):
            begin(j != ten, rcopy(source(j), dest.at[ten], ten_s.at[k, j], ten_r.at[k, ten], ten_dev(j)))

    def collect_ten(k, dest):
        for j in range(n_t):
            @pl.when(j != ten)
            def _():
                rcopy(dest.at[j], dest.at[j], ten_s.at[k, j], ten_r.at[k, j], ten_dev(j)).wait_recv()

    wq_at = lambda b: wq_v.at[b]
    wl_at = lambda b: wl_v.at[b, core]
    we_at = lambda b: we_v.at[b]
    wo_at = lambda b: wo_v.at[b]
    dq_at = lambda b: dq_v.at[b]
    de_at = lambda b: de_v.at[b]
    dl_at = lambda b: dl_v.at[ten, b]

    own_v[:, :wcol] = jnp.broadcast_to(gain_ref[...].astype(F32), (8, wcol))
    own_v[:, wcol:] = jnp.broadcast_to(lgain_ref[...].astype(F32), (8, ccol))
    spread_dp(0, lambda j: own_v, sm_v)
    sm_v[me] = own_v[...]
    line_start(0, wq_ref, wq_at)
    line_start(1, wl_ref.at[pl.ds(pl.multiple_of(core * half, half), half)], wl_at)
    line_start(2, we_ref, we_at)
    line_start(3, wo_ref, wo_at)
    owns = [
        pltpu.make_async_copy(wq_ref, wq_v.at[me], own_sem.at[0]),
        pltpu.make_async_copy(wl_ref.at[pl.ds(0, half)], wl_v.at[me, 0], own_sem.at[1]),
        pltpu.make_async_copy(wl_ref.at[pl.ds(half, half)], wl_v.at[me, 1], own_sem.at[2]),
        pltpu.make_async_copy(we_ref, we_v.at[me], own_sem.at[3]),
        pltpu.make_async_copy(wo_ref, wo_v.at[me], own_sem.at[4]),
    ]
    for copy in owns:
        copy.start()

    for j in range(n_t):
        for m in range(micros):
            x_v[j * share + m * chunk : j * share + (m + 1) * chunk] = saved_ref[
                m, j * chunk : (j + 1) * chunk
            ]
    for copy in owns:
        copy.wait()
    collect_dp(0, sm_v)
    gain = jnp.concatenate([sm_v[d][0:1, :wcol] for d in range(n)], axis=1)
    lgain = jnp.concatenate([sm_v[d][0:1, wcol : wcol + ccol] for d in range(n)], axis=1)
    x32 = x_v[...].astype(F32)
    r = lax.rsqrt(jnp.mean(x32 * x32, axis=1, keepdims=True) + EPS)
    nb = (x32 * r * gain).astype(BF)
    nb_v[...] = nb

    pair_copies = []

    def to_partner(block, valid, way, s):
        copy = rcopy(wl_v.at[block, core], wl_v.at[block, core], pair_s.at[block], pair_r.at[block], ten_dev(partner))
        begin(valid, copy)
        pair_copies.append((valid, block))

    def cols(b):
        return pl.ds(pl.multiple_of(b * wcol, wcol), wcol)

    def use_query(b):
        q_v[...] += mm(nb_v[:, cols(b)], wq_v[b])

    def use_latent(b):
        lat_v[...] += mm_nt(nb_v[:, cols(b)], wl_v[b].reshape(2 * half, wcol))

    last = sec == n_pipe - 1

    @pl.when(last)
    def _():
        for j in range(n_t):
            for m in range(micros):
                u_v[j, m * chunk : (m + 1) * chunk] = top_ref[m, j * chunk : (j + 1) * chunk]

    q_v[...] = mm(nb_v[:, cols(me)], wq_v[me])
    lat_v[...] = mm_nt(nb_v[:, cols(me)], wl_v[me].reshape(2 * half, wcol))

    def settle_latent(pairs):
        for valid, block in pairs:
            @pl.when(valid)
            def _(block=block):
                rcopy(
                    wl_v.at[block, 1 - core], wl_v.at[block, 1 - core], pair_s.at[block], pair_r.at[block], ten_dev(partner)
                ).wait_recv()
                use_latent(block)

    for s in range(n - 1):
        line_step(0, wq_at, s)
        line_step(1, wl_at, s, to_partner)
        for valid, block in pair_copies[-2:]:
            @pl.when(valid)
            def _(block=block):
                use_query(block)

        line_step(2, we_at, s)
        line_step(3, wo_at, s)
        settle_latent(pair_copies[-2:])

    wq = wq_v[...].reshape(width, wq_v.shape[2])
    wl = [wl_v[d].reshape(2 * half, wcol) for d in range(n)]
    we = we_v[...].reshape(n * ccol, we_v.shape[2])
    q = q_v[...]
    lat = lat_v[...]
    rank = n * ccol
    l32 = lat[:, :rank]
    rl = lax.rsqrt(jnp.mean(l32 * l32, axis=1, keepdims=True) + EPS)
    cb = (l32 * rl * lgain).astype(BF)
    cb_v[...] = cb
    spread_dp(1, lambda j: nb_v.at[:, pl.ds(j * wcol, wcol)], nc_v)
    spread_dp(2, lambda j: cb_v.at[:, pl.ds(j * ccol, ccol)], cc_v)
    ex = mm(cb, we)
    cosine, sine = cos_ref[...], sin_ref[...]
    lr = lat[:, rank:]
    lr2 = jnp.concatenate([lr, lr], axis=1)
    rk = (lr2 * cosine + half_swap(lr2) * sine).astype(BF)
    lane = lax.broadcasted_iota(jnp.int32, (rows, 2 * ROPE), 1)
    low = lane < ROPE
    q1, q2 = q[:, NOPE : 2 * NOPE], q[:, 2 * NOPE :]
    nope = (q[:, :NOPE], pltpu.roll(jnp.where(low, q2, q1), ROPE, 1))
    qr_all = jnp.where(low, q1, q2)
    qr = qr_all * cosine + half_swap(qr_all) * sine
    row = lax.broadcasted_iota(jnp.int32, (rows, rows), 0)
    col = lax.broadcasted_iota(jnp.int32, (rows, rows), 1)

    def place(i):
        return (i // share) * chunk + lax.rem(i, chunk)

    same = lax.rem(row, share) // chunk == lax.rem(col, share) // chunk
    keep = jnp.logical_and(same, place(row) >= place(col))
    scale = (NOPE + ROPE) ** (-0.5)
    heads = []
    for h in range(2):
        qn = nope[h].astype(BF)
        kn = ex[:, h * (NOPE + VDIM) : h * (NOPE + VDIM) + NOPE].astype(BF)
        vv = ex[:, h * (NOPE + VDIM) + NOPE : (h + 1) * (NOPE + VDIM)].astype(BF)
        mask = low if h == 0 else jnp.logical_not(low)
        qh = jnp.where(mask, qr, 0.0).astype(BF)
        scores = (mm_nt(qn, kn) + mm_nt(qh, rk)) * scale
        scores = jnp.where(keep, scores, -1e30)
        e = jnp.exp(scores - jnp.max(scores, axis=1, keepdims=True))
        w32 = e / jnp.sum(e, axis=1, keepdims=True)
        wb = w32.astype(BF)
        mx_v[me, :, h * VDIM : (h + 1) * VDIM] = mm(wb, vv).astype(BF)
        heads.append((qn, kn, vv, mask, qh, w32, wb))
    spread_dp(3, lambda j: mx_v.at[me], mx_v)
    for j in range(n):
        @pl.when(j == me)
        def _():
            nc_v[j] = nb_v[:, j * wcol : (j + 1) * wcol]
            cc_v[j] = cb_v[:, j * ccol : (j + 1) * ccol]

    for j in range(n_t):
        @pl.when(sec < n_pipe - 1)
        def _():
            rcopy(
                u_v.at[j], u_v.at[j], pipe_s.at[j], pipe_r.at[j], (jnp.minimum(sec + 1, n_pipe - 1), me, j)
            ).wait_recv()

    ub = u_v[...].reshape(rows, width)
    for j in range(n):
        uc_v[1, j] = ub[:, j * wcol : (j + 1) * wcol]
    spread_dp(4, lambda j: uc_v.at[1, j], uc_v.at[0])
    uc_v[0, me] = uc_v[1, me]
    dm = jnp.zeros((rows, wo_v.shape[1]), F32)
    for j in range(n):
        dm = dm + mm_nt(ub[:, j * wcol : (j + 1) * wcol], wo_v[j])
    dm = dm.astype(BF)
    dqr = jnp.zeros((rows, 2 * ROPE), F32)
    drk = jnp.zeros((rows, 2 * ROPE), F32)
    dqn = []
    for h, (qn, kn, vv, mask, qh, w32, wb) in enumerate(heads):
        dmh = dm[:, h * VDIM : (h + 1) * VDIM]
        dv = mm_tn(wb, dmh)
        dw = mm_nt(dmh, vv).astype(BF).astype(F32)
        ds = (w32 * (dw - jnp.sum(dw * w32, axis=1, keepdims=True)) * scale).astype(BF)
        dqn.append(mm(ds, kn))
        dqr = dqr + jnp.where(mask, mm(ds, rk), 0.0)
        drk = drk + mm_tn(ds, qh)
        de_v[me, :, h * (NOPE + VDIM) : h * (NOPE + VDIM) + NOPE] = mm_tn(ds, qn).astype(BF)
        de_v[me, :, h * (NOPE + VDIM) + NOPE : (h + 1) * (NOPE + VDIM)] = dv.astype(BF)
    dqr = dqr * cosine - half_swap(dqr) * sine
    turned = pltpu.roll(dqn[1], ROPE, 1)
    dq_v[me, :, :NOPE] = dqn[0].astype(BF)
    dq_v[me, :, NOPE : 2 * NOPE] = jnp.where(low, dqr, turned).astype(BF)
    dq_v[me, :, 2 * NOPE :] = jnp.where(low, turned, dqr).astype(BF)
    drk = drk * cosine - half_swap(drk) * sine
    drk = drk + pltpu.roll(drk, ROPE, 1)
    line_start(4, dq_v.at[me], dq_at)
    line_start(5, de_v.at[me], de_at)
    dc = mm_nt(de_v[me], we)
    dlg = jnp.sum(dc * l32 * rl, axis=0, keepdims=True)
    dcg = dc * lgain
    dl = rl * dcg - l32 * (rl * rl * rl) * jnp.mean(l32 * dcg, axis=1, keepdims=True)
    dlat = jnp.concatenate([dl.astype(BF), drk[:, :ROPE].astype(BF)], axis=1)
    dn = mm_nt(dq_v[me], wq) + jnp.concatenate([mm(dlat, wl[d]) for d in range(n)], axis=1)
    part_v[...] = dn.astype(BF).reshape(n_t, share, width)
    spread_ten(0, lambda j: part_v.at[j], rs_v)
    lp_v[...] = dlat.reshape(n_t, share, dlat.shape[1])
    spread_ten(3, lambda j: lp_v.at[j], ls_v)
    rs_v[ten] = part_v[ten]
    ls_v[ten] = lp_v[ten]
    bottom = sec == 0
    line_step(4, dq_at, 0, gate=bottom)
    line_step(5, de_at, 0, gate=bottom)
    collect_ten(0, rs_v)
    dns = jnp.sum(rs_v[...].astype(F32), axis=0)
    x_my = x_v[pl.ds(pl.multiple_of(ten * share, share), share)].astype(F32)
    r_my = lax.rsqrt(jnp.mean(x_my * x_my, axis=1, keepdims=True) + EPS)
    dng = dns * gain
    u_my = u_v[ten].astype(F32)
    dx = u_my + r_my * dng - x_my * (r_my * r_my * r_my) * jnp.mean(x_my * dng, axis=1, keepdims=True)
    dx_v[...] = dx.astype(BF)
    for j in range(n_t):
        begin(sec > 0, rcopy(dx_v, u_v.at[ten], pipe_s.at[j], pipe_r.at[ten], (jnp.maximum(sec - 1, 0), me, j)))
    collect_ten(3, ls_v)
    dl_v[ten, me] = jnp.sum(ls_v[...].astype(F32), axis=0).astype(BF)
    line_start(6, dl_v.at[ten, me], dl_at)
    dgain = jnp.sum(dns * x_my * r_my, axis=0, keepdims=True)
    for j in range(n):
        piece = jnp.concatenate(
            [dgain[:, j * wcol : (j + 1) * wcol], dlg[:, j * ccol : (j + 1) * ccol]], axis=1
        )
        sg_v[j] = jnp.broadcast_to(piece, sg_v.shape[1:])
    spread_dp(5, lambda j: sg_v.at[j], sr_v)
    sr_v[me] = sg_v[me]

    def to_tensor(block, valid=None, way=0, s=0):
        for j in range(n_t):
            cond = j != ten if valid is None else jnp.logical_and(valid, j != ten)
            begin(
                cond,
                rcopy(dl_v.at[ten, block], dl_v.at[ten, block], lat_s.at[j, block], lat_r.at[ten, block], ten_dev(j)),
            )

    to_tensor(me)
    line_step(4, dq_at, 0, gate=sec > 0)
    line_step(5, de_at, 0, gate=sec > 0)
    for m in range(micros):
        ig_ref[m] = dx[m * chunk : (m + 1) * chunk].astype(BF)
    for s in range(1, n - 1):
        line_step(6, dl_at, s - 1, to_tensor)
        line_step(4, dq_at, s)
        line_step(5, de_at, s)
    line_step(6, dl_at, n - 2, to_tensor)
    collect_dp(5, sr_v)
    st_v[ten] = jnp.sum(sr_v[...], axis=0)
    spread_ten(2, lambda j: st_v.at[ten], st_v)
    collect_dp(1, nc_v)
    collect_dp(2, cc_v)
    collect_dp(3, mx_v)
    collect_dp(4, uc_v.at[0])
    nc = nc_v[...].reshape(n * rows, wcol)
    gq_ref[...] = mm_tn(nc, dq_v[...].reshape(n * rows, dq_v.shape[2]))
    ge_ref[...] = mm_tn(cc_v[...].reshape(n * rows, ccol), de_v[...].reshape(n * rows, de_v.shape[2]))
    go_ref[...] = mm_tn(mx_v[...].reshape(n * rows, mx_v.shape[2]), uc_v[0].reshape(n * rows, wcol))
    for j in range(n_t):
        for d in range(n):
            @pl.when(j != ten)
            def _():
                rcopy(dl_v.at[j, d], dl_v.at[j, d], lat_s.at[j, d], lat_r.at[j, d], ten_dev(j)).wait_recv()

    acc = jnp.zeros(gl_ref.shape, F32)
    for d in range(n):
        block = jnp.concatenate([dl_v[j, d] for j in range(n_t)], axis=0)
        acc = acc + mm_tn(block, nc_v[d])
    gl_ref[...] = acc
    collect_ten(2, st_v)
    summed = jnp.sum(st_v[...], axis=0)
    gg_ref[...] = summed[0:1, :wcol]
    glg_ref[...] = summed[0:1, wcol:]
    for cond, copy in drains:
        @pl.when(cond)
        def _(copy=copy):
            copy.wait_send()


def hand_over(*refs):
    for source, dest in zip(refs[:7], refs[7:]):
        dest[...] = source[...]


def section_step(saved, top_grad, gain, w_query, w_latent, compressed_gain, expand_weight, w_output):
    n_pipe, n, n_t = (lax.axis_size(a) for a in ("pipe", "dp", "tensor"))
    micros, seq, width = saved.shape[1:]
    wcol, ccol = gain.shape[1], compressed_gain.shape[1]
    rows, share = micros * seq, micros * seq // n_t
    qcols, lcols = w_query.shape[2], w_latent.shape[2]
    ecols, orows = expand_weight.shape[2], w_output.shape[1]
    order = np.arange(rows)
    place = (order // share) * (seq // n_t) + order % (seq // n_t)
    pair = np.arange(2 * ROPE) % (ROPE // 2)
    angle = place[:, None] * np.exp(-np.log(10000.0) * pair / (ROPE // 2))[None, :]
    sign = np.where(np.arange(2 * ROPE) % ROPE < ROPE // 2, -1.0, 1.0)
    cosine = jnp.asarray(np.cos(angle), F32)
    sine = jnp.asarray(np.sin(angle) * sign, F32)
    vm = pl.BlockSpec(memory_space=pltpu.VMEM)
    shape = jax.ShapeDtypeStruct
    dma = pltpu.SemaphoreType.DMA
    ig, gg, gq, gl, glg, ge, go = pl.pallas_call(
        lambda *refs: section_kernel((n_pipe, n, n_t, micros, seq), *refs),
        name="section_step",
        out_shape=(
            shape((micros, seq // n_t, width), BF),
            shape((1, wcol), F32),
            shape((wcol, qcols), F32),
            shape((lcols, wcol), F32),
            shape((1, ccol), F32),
            shape((ccol, ecols), F32),
            shape((orows, wcol), F32),
        ),
        in_specs=[vm] * 10,
        out_specs=(vm,) * 7,
        scratch_shapes=[
            pltpu.VMEM((rows, width), BF),
            pltpu.VMEM((8, wcol + ccol), F32),
            pltpu.VMEM((n_t, share, width), BF),
            pltpu.VMEM((rows, width), BF),
            pltpu.VMEM((rows, n * ccol), BF),
            pltpu.VMEM((n, 8, wcol + ccol), F32),
            pltpu.VMEM((n, wcol, qcols), BF),
            pltpu.VMEM((n, 2, lcols // 2, wcol), BF),
            pltpu.VMEM((n, ccol, ecols), BF),
            pltpu.VMEM((n, orows, wcol), BF),
            pltpu.VMEM((n, rows, wcol), BF),
            pltpu.VMEM((n, rows, ccol), BF),
            pltpu.VMEM((n, rows, orows), BF),
            pltpu.VMEM((2, n, rows, wcol), BF),
            pltpu.VMEM((n, rows, qcols), BF),
            pltpu.VMEM((n, rows, ecols), BF),
            pltpu.VMEM((n_t, n, share, lcols), BF),
            pltpu.VMEM((n_t, share, width), BF),
            pltpu.VMEM((n_t, share, width), BF),
            pltpu.VMEM((n_t, share, lcols), BF),
            pltpu.VMEM((n_t, share, lcols), BF),
            pltpu.VMEM((rows, qcols), F32),
            pltpu.VMEM((rows, lcols), F32),
            pltpu.VMEM((share, width), BF),
            pltpu.VMEM((n, 8, wcol + ccol), F32),
            pltpu.VMEM((n, 8, wcol + ccol), F32),
            pltpu.VMEM((n_t, 8, wcol + ccol), F32),
            dma((6,)),
            dma((7, 2, n)),
            dma((7, n)),
            dma((n,)),
            dma((n,)),
            dma((6, n)),
            dma((6, n)),
            dma((4, n_t)),
            dma((4, n_t)),
            dma((n_t,)),
            dma((n_t,)),
            dma((n_t, n)),
            dma((n_t, n)),
        ],
        compiler_params=pltpu.CompilerParams(
            collective_id=0, has_side_effects=True, vmem_limit_bytes=60 * 1024 * 1024
        ),
    )(
        saved[0], top_grad, gain, compressed_gain, w_query[0], w_latent[0].T,
        expand_weight[0], w_output[0], cosine, sine,
    )
    parts = (ig, gg, gq, gl, glg, ge, go)
    ig, gg, gq, gl, glg, ge, go = pl.pallas_call(
        hand_over,
        name="hand_over",
        out_shape=tuple(shape(p.shape, p.dtype) for p in parts),
        in_specs=[vm] * 7,
        out_specs=(vm,) * 7,
    )(*parts)
    return ig[None], gg, gq[None], gl.T[None], glg, ge[None], go[None]


def choose(saved, top_grad, gain, w_query, w_latent, compressed_gain, expand_weight, w_output):
    arrays = (saved, top_grad, gain, w_query, w_latent, compressed_gain, expand_weight, w_output)
    n_t = lax.axis_size("tensor")
    fits = (
        lax.axis_size("dp") > 1
        and n_t % 2 == 0
        and w_query.shape[2] == 2 * (NOPE + ROPE)
        and gain.shape[1] % 128 == 0
        and compressed_gain.shape[1] % 128 == 0
        and saved.shape[2] % (16 * n_t) == 0
    )
    return section_step(*arrays) if fits else shards(*arrays)


def solution(mesh):
    in_specs = (
        P("pipe", None, "dp", None),
        P(None, "dp", None),
        P("pipe", "dp"),
        P("pipe", "dp", "tensor"),
        P("pipe", "dp", None),
        P("pipe", "dp"),
        P("pipe", "dp", "tensor"),
        P("pipe", "tensor", "dp"),
    )
    out_specs = (
        P("pipe", None, ("dp", "tensor"), None),
        P("pipe", "dp"),
        P("pipe", "dp", "tensor"),
        P("pipe", "dp", None),
        P("pipe", "dp"),
        P("pipe", "dp", "tensor"),
        P("pipe", "tensor", "dp"),
    )
    return jax.shard_map(choose, mesh=mesh, in_specs=in_specs, out_specs=out_specs, check_vma=False)
```

profile of v0, /device:TPU:0, one launch (start us, length us, event | category | flops | bytes accessed | tf_op | source)
XLA Modules:
  0.0 103.7 jit_solution(9494235014352837012)
XLA Ops:
  0.6 100.6 %section_step.1 = (bf16[2,16,1024]{2,1,0:T(8,128)(2,1)}, f32[1,256]{1,0:T(1,128)}, f32[256,384]{1,0:T(8,128)}, f32[576,256]{1,0:T(8,128)}, f32[1,128]{1,0:T(1,12...) custom-call(bf16[2,64,1024]{2,1,0:T(8,128)(2,1)} %bitcast.15, bf16[2,64,1024]{2,1,0:T(8,128)(2,1)} %refs_1_.1, ...), custom_call_target="tpu_custom_call" | custom-call | tf_op jit(solution)/shard_map/section_step/pallas_call | solution.py:607
  101.2 2.5 %hand_over.1 = (bf16[2,16,1024]{2,1,0:T(8,128)(2,1)}, f32[1,256]{1,0:T(1,128)}, f32[256,384]{1,0:T(8,128)}, f32[576,256]{1,0:T(8,128)}, f32[1,128]{1,0:T(1,128)}...) custom-call(bf16[2,16,1024]{2,1,0:T(8,128)(2,1)} %get-tuple-element.21.refs_0_, f32[1,256]{1,0:T(1,128)} %get-tuple-element.22.refs_1_, ...), custom_call_target="tpu_custom_call" | custom-call | tf_op jit(solution)/shard_map/hand_over/pallas_call | solution.py:671
where the time goes:
time: 104 us
  Pallas kernels  103 us (99%)
    pallas_call x1, Pallas kernels, section_step(): pl.pallas_call(lambda *refs: section_kernel((n_pipe, n, n_t, micros, seq)...  101 us
    pallas_call x1, Pallas kernels, section_step(): pl.pallas_call(hand_over, name='hand_over', out_shape=tuple((shape(p.shap...  2.54 us

commit v1 on v0

--- a/solution.py
+++ b/solution.py
@@ -216,9 +216,11 @@
     dims,
     saved_ref, top_ref, gain_ref, lgain_ref, wq_ref, wl_ref, we_ref, wo_ref, cos_ref, sin_ref,
     ig_ref, gg_ref, gq_ref, gl_ref, glg_ref, ge_ref, go_ref,
-    x_v, own_v, u_v, nb_v, cb_v, sm_v, wq_v, wl_v, we_v, wo_v,
-    nc_v, cc_v, mx_v, uc_v, dq_v, de_v, dl_v, part_v, rs_v, lp_v, ls_v, q_v, lat_v, dx_v, sg_v, sr_v, st_v,
-    own_sem, line_s, line_r, pair_s, pair_r, dp_s, dp_r, ten_s, ten_r, pipe_s, pipe_r, lat_s, lat_r,
+    x_v, xs_v, own_v, sm_v, nm_v, u_v, um_v, cb_v, wq_v, wl_v, we_v, wo_v,
+    nc_v, cc_v, uc_v, dl_v, fo_v, fw_v, so_v, sv_v, part_v, rs_v, lp_v, ls_v, dx_v, sg_v, sr_v, st_v,
+    dq_v, de_v,
+    dp_s, dp_r, x_s, x_r, line_s, line_r, wt_s, wt_r, w_s, w_r, f_s, f_r, z_s, z_r, t_s, t_r,
+    b_s, b_r, rs_s, rs_r, p_s, u_r, um_r, uf_s, uf_r, st_s, st_r,
 ):
     n_pipe, n, n_t, micros, seq = dims
     sec, me, ten = lax.axis_index("pipe"), lax.axis_index("dp"), lax.axis_index("tensor")
@@ -226,11 +228,20 @@
     chunk = seq // n_t
     share = micros * chunk
     width = x_v.shape[1]
-    wcol = wq_v.shape[1]
-    ccol = we_v.shape[1]
+    wcol, ccol = wq_v.shape[1], we_v.shape[1]
+    rank = n * ccol
+    quarter = wl_v.shape[2]
     core = lax.rem(ten, 2)
     partner = ten + 1 - 2 * core
-    half = wl_ref.shape[0] // 2
+    par = lax.rem(me, 2)
+    mate = me + 1 - 2 * par
+    group = ten - core + par
+    block = me - par + core
+    primary = core == par
+    secondary = jnp.logical_not(primary)
+    last = sec == n_pipe - 1
+    lower = jnp.logical_not(last)
+    both = jnp.logical_and
     drains = []
 
     def rcopy(a, b, ss, rs, dev):
@@ -245,178 +256,209 @@
 
         drains.append((cond, copy))
 
-    def dp_dev(d):
-        return (sec, d, ten)
-
-    def ten_dev(d):
-        return (sec, me, d)
+    def arrived(cond, ref, rs):
+        @pl.when(cond)
+        def _():
+            rcopy(ref, ref, x_s.at[0], rs, dev(me, partner)).wait_recv()
+
+    def dev(d, t):
+        return (sec, d, t)
+
+    def cols(j, size):
+        return slice(j * size, (j + 1) * size)
+
+    def mine(ref):
+        at = pl.ds(pl.multiple_of(ten * chunk, chunk), chunk)
+        return jnp.concatenate([ref[m, at] for m in range(micros)], axis=0)
+
+    def by_share(store, ref):
+        for j in range(n_t):
+            for m in range(micros):
+                store(j, m, ref[m, j * chunk : (j + 1) * chunk])
+
+    def x_store(j, m, value):
+        x_v[j * share + m * chunk : j * share + (m + 1) * chunk] = value
+
+    def u_store(j, m, value):
+        u_v[j, m * chunk : (m + 1) * chunk] = value
+
+    own_v[:, :wcol] = jnp.broadcast_to(gain_ref[...].astype(F32), (8, wcol))
+    own_v[:, wcol:] = jnp.broadcast_to(lgain_ref[...].astype(F32), (8, ccol))
+
+    @pl.when(last)
+    def _():
+        um_v[...] = mine(top_ref)
+
+    @pl.when(both(last, primary))
+    def _():
+        by_share(u_store, top_ref)
 
     barrier = pltpu.get_barrier_semaphore()
-    for j in range(n):
-        @pl.when(j != me)
-        def _():
-            pl.semaphore_signal(barrier, inc=1, device_id=dp_dev(j), device_id_type=MESH)
-
     for j in range(n_t):
-        @pl.when(j != ten)
-        def _():
-            pl.semaphore_signal(barrier, inc=1, device_id=ten_dev(j), device_id_type=MESH)
+        for d in range(n):
+            @pl.when(jnp.logical_or(d != me, j != ten))
+            def _():
+                pl.semaphore_signal(barrier, inc=1, device_id=dev(d, j), device_id_type=MESH)
 
         @pl.when(sec > 0)
         def _():
             pl.semaphore_signal(barrier, inc=1, device_id=(sec - 1, me, j), device_id_type=MESH)
 
-        @pl.when(sec < n_pipe - 1)
+        @pl.when(lower)
         def _():
             pl.semaphore_signal(barrier, inc=1, device_id=(sec + 1, me, j), device_id_type=MESH)
 
     neighbours = jnp.minimum(sec, 1) + jnp.minimum(n_pipe - 1 - sec, 1)
-    pl.semaphore_wait(barrier, n - 1 + n_t - 1 + neighbours * n_t)
-
-    def line_start(k, source, at):
-        begin(me < n - 1, rcopy(source, at(me), line_s.at[k, 0, 0], line_r.at[k, me], dp_dev(me + 1)))
-        begin(me > 0, rcopy(source, at(me), line_s.at[k, 1, 0], line_r.at[k, me], dp_dev(me - 1)))
-
-    def line_step(k, at, s, extra=None, gate=None):
-        for way, block, valid, more, dest in (
+    pl.semaphore_wait(barrier, n * n_t - 1 + neighbours * n_t)
+
+    def spread_dp(k, source, dest):
+        for j in range(n):
+            begin(j != me, rcopy(source(j), dest.at[me], dp_s.at[k, j], dp_r.at[k, me], dev(j, ten)))
+
+    def collect_dp(k, dest):
+        for j in range(n):
+            arrived(j != me, dest.at[j], dp_r.at[k, j])
+
+    def spread_z(k, source, dest, slot, rank_to, gate=None):
+        for e in range(n):
+            cond = jnp.logical_or(e != me, rank_to != ten)
+            if gate is not None:
+                cond = both(cond, gate)
+            begin(cond, rcopy(source(e), dest.at[slot, rank_to], z_s.at[k, e], z_r.at[k, slot], dev(e, rank_to)))
+
+    def relay(k, dest, owned=None):
+        for b in range(n):
+            here = b == me if owned is None else both(b == me, owned)
+            arrived(jnp.logical_not(here), dest.at[b, ten], z_r.at[k, b])
+            for j in range(n_t):
+                begin(
+                    j != ten,
+                    rcopy(dest.at[b, ten], dest.at[b, ten], t_s.at[k, b, j], t_r.at[k, b, ten], dev(me, j)),
+                )
+
+    def collect(k, dest):
+        for b in range(n):
+            for j in range(n_t):
+                arrived(j != ten, dest.at[b, j], t_r.at[k, b, j])
+
+    def spread_block(k, source, dest, gate=None):
+        for e in range(n):
+            cond = jnp.logical_or(e != me, secondary)
+            if gate is not None:
+                cond = both(cond, gate)
+            begin(cond, rcopy(source, dest.at[block], b_s.at[k, e], b_r.at[k, block], dev(e, group)))
+
+    def collect_block(k, dest):
+        for b in range(n):
+            arrived(jnp.logical_or(b != me, secondary), dest.at[b], b_r.at[k, b])
+
+    def line_start(source, at):
+        begin(me < n - 1, rcopy(source, at(me), line_s.at[0, 0], line_r.at[me], dev(me + 1, ten)))
+        begin(me > 0, rcopy(source, at(me), line_s.at[1, 0], line_r.at[me], dev(me - 1, ten)))
+
+    def line_step(at, s, extra):
+        for way, b, valid, more, dest in (
             (0, jnp.maximum(me - 1 - s, 0), me - 1 - s >= 0, me < n - 1, me + 1),
             (1, jnp.minimum(me + 1 + s, n - 1), me + 1 + s <= n - 1, me > 0, me - 1),
         ):
-            if gate is not None:
-                valid = jnp.logical_and(valid, gate)
-            arrived = rcopy(at(block), at(block), line_s.at[k, way, s + 1], line_r.at[k, block], dp_dev(dest))
+            copy = rcopy(at(b), at(b), line_s.at[way, s + 1], line_r.at[b], dev(dest, ten))
 
             @pl.when(valid)
             def _():
-                arrived.wait_recv()
+                copy.wait_recv()
 
             if s < n - 2:
-                begin(jnp.logical_and(valid, more), arrived)
-            if extra is not None:
-                extra(block, valid, way, s)
-
-    def spread_dp(k, source, dest):
-        for j in range(n):
-            begin(j != me, rcopy(source(j), dest.at[me], dp_s.at[k, j], dp_r.at[k, me], dp_dev(j)))
-
-    def collect_dp(k, dest):
-        for j in range(n):
-            @pl.when(j != me)
-            def _():
-                rcopy(dest.at[j], dest.at[j], dp_s.at[k, j], dp_r.at[k, j], dp_dev(j)).wait_recv()
-
-    def spread_ten(k, source, dest):
-        for j in range(n_t):
-            begin(j != ten, rcopy(source(j), dest.at[ten], ten_s.at[k, j], ten_r.at[k, ten], ten_dev(j)))
-
-    def collect_ten(k, dest):
-        for j in range(n_t):
-            @pl.when(j != ten)
-            def _():
-                rcopy(dest.at[j], dest.at[j], ten_s.at[k, j], ten_r.at[k, j], ten_dev(j)).wait_recv()
-
-    wq_at = lambda b: wq_v.at[b]
-    wl_at = lambda b: wl_v.at[b, core]
-    we_at = lambda b: we_v.at[b]
-    wo_at = lambda b: wo_v.at[b]
-    dq_at = lambda b: dq_v.at[b]
-    de_at = lambda b: de_v.at[b]
-    dl_at = lambda b: dl_v.at[ten, b]
-
-    own_v[:, :wcol] = jnp.broadcast_to(gain_ref[...].astype(F32), (8, wcol))
-    own_v[:, wcol:] = jnp.broadcast_to(lgain_ref[...].astype(F32), (8, ccol))
+                begin(both(valid, more), copy)
+            extra(b, valid)
+
     spread_dp(0, lambda j: own_v, sm_v)
     sm_v[me] = own_v[...]
-    line_start(0, wq_ref, wq_at)
-    line_start(1, wl_ref.at[pl.ds(pl.multiple_of(core * half, half), half)], wl_at)
-    line_start(2, we_ref, we_at)
-    line_start(3, wo_ref, wo_at)
-    owns = [
-        pltpu.make_async_copy(wq_ref, wq_v.at[me], own_sem.at[0]),
-        pltpu.make_async_copy(wl_ref.at[pl.ds(0, half)], wl_v.at[me, 0], own_sem.at[1]),
-        pltpu.make_async_copy(wl_ref.at[pl.ds(half, half)], wl_v.at[me, 1], own_sem.at[2]),
-        pltpu.make_async_copy(we_ref, we_v.at[me], own_sem.at[3]),
-        pltpu.make_async_copy(wo_ref, wo_v.at[me], own_sem.at[4]),
-    ]
-    for copy in owns:
-        copy.start()
+    begin(primary, rcopy(saved_ref, xs_v, x_s.at[0], x_r.at[0], dev(mate, ten)))
+    line_start(
+        wl_ref.at[pl.ds(pl.multiple_of(ten * quarter, quarter), quarter)], lambda b: wl_v.at[b, ten]
+    )
+    weights = ((wq_ref, wq_v), (we_ref, we_v), (wo_ref, wo_v))
+    for k, (ref, store) in enumerate(weights):
+        for i in range(n // 2):
+            level = 2 * i + core
+            begin(level != me, rcopy(ref, store.at[me], w_s.at[k, i], w_r.at[k, me], dev(level, ten)))
+        begin(primary, rcopy(ref, store.at[me], f_s.at[k, me], f_r.at[k, me], dev(me, partner)))
+    for s in range(n_t):
+        begin(both(last, primary), rcopy(u_v.at[s], u_v.at[s], uf_s.at[s], uf_r.at[s], dev(mate, ten)))
+    um_cols = lambda e: um_v.at[:, pl.ds(e * wcol, wcol)]
+    spread_z(2, um_cols, uc_v, me, ten, gate=last)
 
     for j in range(n_t):
-        for m in range(micros):
-            x_v[j * share + m * chunk : j * share + (m + 1) * chunk] = saved_ref[
-                m, j * chunk : (j + 1) * chunk
-            ]
-    for copy in owns:
-        copy.wait()
+        wl_v[me, j] = wl_ref[j * quarter : (j + 1) * quarter]
+
+    @pl.when(primary)
+    def _():
+        for ref, store in weights:
+            store[me] = ref[...]
+
+        by_share(x_store, saved_ref)
+
     collect_dp(0, sm_v)
     gain = jnp.concatenate([sm_v[d][0:1, :wcol] for d in range(n)], axis=1)
     lgain = jnp.concatenate([sm_v[d][0:1, wcol : wcol + ccol] for d in range(n)], axis=1)
+    x_my = mine(saved_ref).astype(F32)
+    r_my = lax.rsqrt(jnp.mean(x_my * x_my, axis=1, keepdims=True) + EPS)
+    nm_v[...] = (x_my * r_my * gain).astype(BF)
+    spread_z(0, lambda e: nm_v.at[:, pl.ds(e * wcol, wcol)], nc_v, me, ten)
+    for j in range(n):
+        @pl.when(j == me)
+        def _():
+            nc_v[j, ten] = nm_v[:, cols(j, wcol)]
+
+    @pl.when(secondary)
+    def _():
+        rcopy(xs_v, xs_v, x_s.at[0], x_r.at[0], dev(me, partner)).wait_recv()
+        by_share(x_store, xs_v)
+
     x32 = x_v[...].astype(F32)
     r = lax.rsqrt(jnp.mean(x32 * x32, axis=1, keepdims=True) + EPS)
     nb = (x32 * r * gain).astype(BF)
-    nb_v[...] = nb
-
-    pair_copies = []
-
-    def to_partner(block, valid, way, s):
-        copy = rcopy(wl_v.at[block, core], wl_v.at[block, core], pair_s.at[block], pair_r.at[block], ten_dev(partner))
-        begin(valid, copy)
-        pair_copies.append((valid, block))
-
-    def cols(b):
-        return pl.ds(pl.multiple_of(b * wcol, wcol), wcol)
-
-    def use_query(b):
-        q_v[...] += mm(nb_v[:, cols(b)], wq_v[b])
-
-    def use_latent(b):
-        lat_v[...] += mm_nt(nb_v[:, cols(b)], wl_v[b].reshape(2 * half, wcol))
-
-    last = sec == n_pipe - 1
-
-    @pl.when(last)
-    def _():
+
+    def to_ten(b, valid):
         for j in range(n_t):
-            for m in range(micros):
-                u_v[j, m * chunk : (m + 1) * chunk] = top_ref[m, j * chunk : (j + 1) * chunk]
-
-    q_v[...] = mm(nb_v[:, cols(me)], wq_v[me])
-    lat_v[...] = mm_nt(nb_v[:, cols(me)], wl_v[me].reshape(2 * half, wcol))
-
-    def settle_latent(pairs):
-        for valid, block in pairs:
-            @pl.when(valid)
-            def _(block=block):
-                rcopy(
-                    wl_v.at[block, 1 - core], wl_v.at[block, 1 - core], pair_s.at[block], pair_r.at[block], ten_dev(partner)
-                ).wait_recv()
-                use_latent(block)
+            begin(
+                both(valid, j != ten),
+                rcopy(wl_v.at[b, ten], wl_v.at[b, ten], wt_s.at[b, j], wt_r.at[b, ten], dev(me, j)),
+            )
+
+    def take(k):
+        store = weights[k][1]
+        for d in range(n):
+            cond = both(primary, d != me)
+            arrived(cond, store.at[d], w_r.at[k, d])
+            begin(cond, rcopy(store.at[d], store.at[d], f_s.at[k, d], f_r.at[k, d], dev(me, partner)))
+        for d in range(n):
+            arrived(secondary, store.at[d], f_r.at[k, d])
 
     for s in range(n - 1):
-        line_step(0, wq_at, s)
-        line_step(1, wl_at, s, to_partner)
-        for valid, block in pair_copies[-2:]:
-            @pl.when(valid)
-            def _(block=block):
-                use_query(block)
-
-        line_step(2, we_at, s)
-        line_step(3, wo_at, s)
-        settle_latent(pair_copies[-2:])
+        line_step(lambda b: wl_v.at[b, ten], s, to_ten)
+    take(0)
+    for d in range(n):
+        for j in range(n_t):
+            arrived(both(d != me, j != ten), wl_v.at[d, j], wt_r.at[d, j])
 
     wq = wq_v[...].reshape(width, wq_v.shape[2])
-    wl = [wl_v[d].reshape(2 * half, wcol) for d in range(n)]
-    we = we_v[...].reshape(n * ccol, we_v.shape[2])
-    q = q_v[...]
-    lat = lat_v[...]
-    rank = n * ccol
+    wl = [wl_v[d].reshape(n_t * quarter, wcol) for d in range(n)]
+    q = mm(nb, wq)
+    lat = jnp.zeros((rows, n_t * quarter), F32)
+    for d in range(n):
+        lat = lat + mm_nt(nb[:, cols(d, wcol)], wl[d])
     l32 = lat[:, :rank]
     rl = lax.rsqrt(jnp.mean(l32 * l32, axis=1, keepdims=True) + EPS)
     cb = (l32 * rl * lgain).astype(BF)
     cb_v[...] = cb
-    spread_dp(1, lambda j: nb_v.at[:, pl.ds(j * wcol, wcol)], nc_v)
-    spread_dp(2, lambda j: cb_v.at[:, pl.ds(j * ccol, ccol)], cc_v)
-    ex = mm(cb, we)
+    my_rows = pl.ds(pl.multiple_of(group * share, share), share)
+    spread_z(1, lambda e: cb_v.at[my_rows, pl.ds(e * ccol, ccol)], cc_v, block, group)
+    for j in range(n):
+        @pl.when(both(j == me, primary))
+        def _():
+            cc_v[j, ten] = cb_v[my_rows, cols(j, ccol)]
+
     cosine, sine = cos_ref[...], sin_ref[...]
     lr = lat[:, rank:]
     lr2 = jnp.concatenate([lr, lr], axis=1)
@@ -435,144 +477,168 @@
 
     same = lax.rem(row, share) // chunk == lax.rem(col, share) // chunk
     keep = jnp.logical_and(same, place(row) >= place(col))
+    picks = [jnp.where(place(row) + h * seq == col, 1.0, 0.0).astype(BF) for h in range(2)]
     scale = (NOPE + ROPE) ** (-0.5)
+    masks = (low, jnp.logical_not(low))
+    take(1)
+    we = we_v[...].reshape(n * ccol, we_v.shape[2])
+    ex = mm(cb, we)
     heads = []
     for h in range(2):
         qn = nope[h].astype(BF)
         kn = ex[:, h * (NOPE + VDIM) : h * (NOPE + VDIM) + NOPE].astype(BF)
         vv = ex[:, h * (NOPE + VDIM) + NOPE : (h + 1) * (NOPE + VDIM)].astype(BF)
-        mask = low if h == 0 else jnp.logical_not(low)
-        qh = jnp.where(mask, qr, 0.0).astype(BF)
+        qh = jnp.where(masks[h], qr, 0.0).astype(BF)
         scores = (mm_nt(qn, kn) + mm_nt(qh, rk)) * scale
         scores = jnp.where(keep, scores, -1e30)
         e = jnp.exp(scores - jnp.max(scores, axis=1, keepdims=True))
         w32 = e / jnp.sum(e, axis=1, keepdims=True)
         wb = w32.astype(BF)
-        mx_v[me, :, h * VDIM : (h + 1) * VDIM] = mm(wb, vv).astype(BF)
-        heads.append((qn, kn, vv, mask, qh, w32, wb))
-    spread_dp(3, lambda j: mx_v.at[me], mx_v)
+        fo_v[:, cols(h, NOPE)] = qn
+        fo_v[:, cols(2 + h, NOPE)] = kn
+        fo_v[:, cols(5 + h, VDIM)] = mm(wb, vv).astype(BF)
+        heads.append((qn, kn, vv, qh, w32, wb))
+    fo_v[:, cols(4, NOPE)] = rk
+
+    @pl.when(primary)
+    def _():
+        fw_v[me] = fo_v[...]
+
+    spread_block(0, fo_v, fw_v, gate=lower)
+    take(2)
+
+    for s in range(n_t):
+        cond = both(lower, primary)
+        arrived(cond, u_v.at[s], u_r.at[s])
+        begin(cond, rcopy(u_v.at[s], u_v.at[s], uf_s.at[s], uf_r.at[s], dev(mate, ten)))
+
+    @pl.when(both(lower, primary))
+    def _():
+        um_v[...] = u_v[ten]
+
+    arrived(both(lower, secondary), um_v, um_r.at[0])
+    spread_z(2, um_cols, uc_v, me, ten, gate=lower)
     for j in range(n):
         @pl.when(j == me)
         def _():
-            nc_v[j] = nb_v[:, j * wcol : (j + 1) * wcol]
-            cc_v[j] = cb_v[:, j * ccol : (j + 1) * ccol]
-
-    for j in range(n_t):
-        @pl.when(sec < n_pipe - 1)
-        def _():
-            rcopy(
-                u_v.at[j], u_v.at[j], pipe_s.at[j], pipe_r.at[j], (jnp.minimum(sec + 1, n_pipe - 1), me, j)
-            ).wait_recv()
+            uc_v[j, ten] = um_v[:, cols(j, wcol)]
+
+    for s in range(n_t):
+        arrived(secondary, u_v.at[s], uf_r.at[s])
 
     ub = u_v[...].reshape(rows, width)
-    for j in range(n):
-        uc_v[1, j] = ub[:, j * wcol : (j + 1) * wcol]
-    spread_dp(4, lambda j: uc_v.at[1, j], uc_v.at[0])
-    uc_v[0, me] = uc_v[1, me]
     dm = jnp.zeros((rows, wo_v.shape[1]), F32)
     for j in range(n):
-        dm = dm + mm_nt(ub[:, j * wcol : (j + 1) * wcol], wo_v[j])
+        dm = dm + mm_nt(ub[:, cols(j, wcol)], wo_v[j])
     dm = dm.astype(BF)
-    dqr = jnp.zeros((rows, 2 * ROPE), F32)
+
+    def query_grad(slope, kn0, kn1, rk_b):
+        dqr = jnp.where(low, mm(slope[0], rk_b), mm(slope[1], rk_b))
+        dqr = dqr * cosine - half_swap(dqr) * sine
+        turned = pltpu.roll(mm(slope[1], kn1), ROPE, 1)
+        return jnp.concatenate(
+            [
+                mm(slope[0], kn0).astype(BF),
+                jnp.where(low, dqr, turned).astype(BF),
+                jnp.where(low, turned, dqr).astype(BF),
+            ],
+            axis=1,
+        )
+
     drk = jnp.zeros((rows, 2 * ROPE), F32)
-    dqn = []
-    for h, (qn, kn, vv, mask, qh, w32, wb) in enumerate(heads):
-        dmh = dm[:, h * VDIM : (h + 1) * VDIM]
-        dv = mm_tn(wb, dmh)
+    slopes, pieces = [], []
+    for h, (qn, kn, vv, qh, w32, wb) in enumerate(heads):
+        dmh = dm[:, cols(h, VDIM)]
         dw = mm_nt(dmh, vv).astype(BF).astype(F32)
         ds = (w32 * (dw - jnp.sum(dw * w32, axis=1, keepdims=True)) * scale).astype(BF)
-        dqn.append(mm(ds, kn))
-        dqr = dqr + jnp.where(mask, mm(ds, rk), 0.0)
         drk = drk + mm_tn(ds, qh)
-        de_v[me, :, h * (NOPE + VDIM) : h * (NOPE + VDIM) + NOPE] = mm_tn(ds, qn).astype(BF)
-        de_v[me, :, h * (NOPE + VDIM) + NOPE : (h + 1) * (NOPE + VDIM)] = dv.astype(BF)
-    dqr = dqr * cosine - half_swap(dqr) * sine
-    turned = pltpu.roll(dqn[1], ROPE, 1)
-    dq_v[me, :, :NOPE] = dqn[0].astype(BF)
-    dq_v[me, :, NOPE : 2 * NOPE] = jnp.where(low, dqr, turned).astype(BF)
-    dq_v[me, :, 2 * NOPE :] = jnp.where(low, turned, dqr).astype(BF)
+        slopes.append(ds)
+        pieces += [mm_tn(ds, qn).astype(BF), mm_tn(wb, dmh).astype(BF)]
     drk = drk * cosine - half_swap(drk) * sine
     drk = drk + pltpu.roll(drk, ROPE, 1)
-    line_start(4, dq_v.at[me], dq_at)
-    line_start(5, de_v.at[me], de_at)
-    dc = mm_nt(de_v[me], we)
+    so_v[:, cols(0, NOPE)] = (mm(slopes[0], picks[0]) + mm(slopes[1], picks[1])).astype(BF)
+    so_v[:, cols(1, VDIM)] = pieces[1]
+    so_v[:, cols(2, VDIM)] = pieces[3]
+    dc = mm_nt(jnp.concatenate(pieces, axis=1), we)
     dlg = jnp.sum(dc * l32 * rl, axis=0, keepdims=True)
     dcg = dc * lgain
     dl = rl * dcg - l32 * (rl * rl * rl) * jnp.mean(l32 * dcg, axis=1, keepdims=True)
     dlat = jnp.concatenate([dl.astype(BF), drk[:, :ROPE].astype(BF)], axis=1)
-    dn = mm_nt(dq_v[me], wq) + jnp.concatenate([mm(dlat, wl[d]) for d in range(n)], axis=1)
+    dq = query_grad(slopes, heads[0][1], heads[1][1], rk)
+    dn = mm_nt(dq, wq) + jnp.concatenate([mm(dlat, wl[d]) for d in range(n)], axis=1)
     part_v[...] = dn.astype(BF).reshape(n_t, share, width)
-    spread_ten(0, lambda j: part_v.at[j], rs_v)
     lp_v[...] = dlat.reshape(n_t, share, dlat.shape[1])
-    spread_ten(3, lambda j: lp_v.at[j], ls_v)
-    rs_v[ten] = part_v[ten]
-    ls_v[ten] = lp_v[ten]
-    bottom = sec == 0
-    line_step(4, dq_at, 0, gate=bottom)
-    line_step(5, de_at, 0, gate=bottom)
-    collect_ten(0, rs_v)
+    for k, (source, dest) in enumerate(((part_v, rs_v), (lp_v, ls_v))):
+        for s in range(n_t):
+            begin(
+                jnp.logical_or(s != ten, secondary),
+                rcopy(source.at[s], dest.at[group], rs_s.at[k, s], rs_r.at[k, group], dev(block, s)),
+            )
+
+    @pl.when(primary)
+    def _():
+        rs_v[group] = part_v[ten]
+        ls_v[group] = lp_v[ten]
+        sv_v[me] = so_v[...]
+
+    spread_block(1, so_v, sv_v, gate=lower)
+    relay(0, nc_v)
+    relay(1, cc_v, owned=primary)
+
+    def collect_shares(k, dest):
+        for g in range(n_t):
+            arrived(jnp.logical_or(g != ten, secondary), dest.at[g], rs_r.at[k, g])
+
+    collect_shares(0, rs_v)
     dns = jnp.sum(rs_v[...].astype(F32), axis=0)
-    x_my = x_v[pl.ds(pl.multiple_of(ten * share, share), share)].astype(F32)
-    r_my = lax.rsqrt(jnp.mean(x_my * x_my, axis=1, keepdims=True) + EPS)
     dng = dns * gain
-    u_my = u_v[ten].astype(F32)
+    u_my = um_v[...].astype(F32)
     dx = u_my + r_my * dng - x_my * (r_my * r_my * r_my) * jnp.mean(x_my * dng, axis=1, keepdims=True)
     dx_v[...] = dx.astype(BF)
-    for j in range(n_t):
-        begin(sec > 0, rcopy(dx_v, u_v.at[ten], pipe_s.at[j], pipe_r.at[ten], (jnp.maximum(sec - 1, 0), me, j)))
-    collect_ten(3, ls_v)
-    dl_v[ten, me] = jnp.sum(ls_v[...].astype(F32), axis=0).astype(BF)
-    line_start(6, dl_v.at[ten, me], dl_at)
+    below = jnp.maximum(sec - 1, 0)
+    for i in range(n_t // 2):
+        begin(sec > 0, rcopy(dx_v, u_v.at[ten], p_s.at[i], u_r.at[ten], (below, me, 2 * i + par)))
+    begin(both(sec > 0, secondary), rcopy(dx_v, um_v, p_s.at[n_t // 2], um_r.at[0], (below, me, ten)))
+    collect_shares(1, ls_v)
+    dl_v[me, ten] = jnp.sum(ls_v[...].astype(F32), axis=0).astype(BF)
+    spread_z(3, lambda e: dl_v.at[me, ten], dl_v, me, ten)
     dgain = jnp.sum(dns * x_my * r_my, axis=0, keepdims=True)
     for j in range(n):
-        piece = jnp.concatenate(
-            [dgain[:, j * wcol : (j + 1) * wcol], dlg[:, j * ccol : (j + 1) * ccol]], axis=1
-        )
+        piece = jnp.concatenate([dgain[:, cols(j, wcol)], dlg[:, cols(j, ccol)]], axis=1)
         sg_v[j] = jnp.broadcast_to(piece, sg_v.shape[1:])
-    spread_dp(5, lambda j: sg_v.at[j], sr_v)
+    spread_dp(1, lambda j: sg_v.at[j], sr_v)
     sr_v[me] = sg_v[me]
-
-    def to_tensor(block, valid=None, way=0, s=0):
-        for j in range(n_t):
-            cond = j != ten if valid is None else jnp.logical_and(valid, j != ten)
-            begin(
-                cond,
-                rcopy(dl_v.at[ten, block], dl_v.at[ten, block], lat_s.at[j, block], lat_r.at[ten, block], ten_dev(j)),
-            )
-
-    to_tensor(me)
-    line_step(4, dq_at, 0, gate=sec > 0)
-    line_step(5, de_at, 0, gate=sec > 0)
+    spread_block(1, so_v, sv_v, gate=last)
+    spread_block(0, fo_v, fw_v, gate=last)
     for m in range(micros):
         ig_ref[m] = dx[m * chunk : (m + 1) * chunk].astype(BF)
-    for s in range(1, n - 1):
-        line_step(6, dl_at, s - 1, to_tensor)
-        line_step(4, dq_at, s)
-        line_step(5, de_at, s)
-    line_step(6, dl_at, n - 2, to_tensor)
-    collect_dp(5, sr_v)
+    relay(2, uc_v)
+    relay(3, dl_v)
+    collect_dp(1, sr_v)
     st_v[ten] = jnp.sum(sr_v[...], axis=0)
-    spread_ten(2, lambda j: st_v.at[ten], st_v)
-    collect_dp(1, nc_v)
-    collect_dp(2, cc_v)
-    collect_dp(3, mx_v)
-    collect_dp(4, uc_v.at[0])
-    nc = nc_v[...].reshape(n * rows, wcol)
-    gq_ref[...] = mm_tn(nc, dq_v[...].reshape(n * rows, dq_v.shape[2]))
+    for j in range(n_t):
+        begin(j != ten, rcopy(st_v.at[ten], st_v.at[ten], st_s.at[j], st_r.at[ten], dev(me, j)))
+    collect_block(0, fw_v)
+    collect_block(1, sv_v)
+    for b in range(n):
+        few = sv_v[b, :, :NOPE]
+        ds = [jnp.where(same, mm_nt(few, picks[h]), 0.0).astype(BF) for h in range(2)]
+        part = lambda i: fw_v[b, :, cols(i, NOPE)]
+        dq_v[b] = query_grad(ds, part(2), part(3), part(4))
+        for h in range(2):
+            de_v[b, :, cols(2 * h, NOPE)] = mm_tn(ds[h], part(h)).astype(BF)
+            de_v[b, :, cols(2 * h + 1, NOPE)] = sv_v[b, :, cols(1 + h, VDIM)]
+    collect(0, nc_v)
+    collect(1, cc_v)
+    gq_ref[...] = mm_tn(nc_v[...].reshape(n * rows, wcol), dq_v[...].reshape(n * rows, dq_v.shape[2]))
     ge_ref[...] = mm_tn(cc_v[...].reshape(n * rows, ccol), de_v[...].reshape(n * rows, de_v.shape[2]))
-    go_ref[...] = mm_tn(mx_v[...].reshape(n * rows, mx_v.shape[2]), uc_v[0].reshape(n * rows, wcol))
+    collect(2, uc_v)
+    mixed = fw_v[:, :, 5 * NOPE :].reshape(n * rows, 2 * VDIM)
+    go_ref[...] = mm_tn(mixed, uc_v[...].reshape(n * rows, wcol))
+    collect(3, dl_v)
+    gl_ref[...] = mm_tn(dl_v[...].reshape(n * rows, dl_v.shape[3]), nc_v[...].reshape(n * rows, wcol))
     for j in range(n_t):
-        for d in range(n):
-            @pl.when(j != ten)
-            def _():
-                rcopy(dl_v.at[j, d], dl_v.at[j, d], lat_s.at[j, d], lat_r.at[j, d], ten_dev(j)).wait_recv()
-
-    acc = jnp.zeros(gl_ref.shape, F32)
-    for d in range(n):
-        block = jnp.concatenate([dl_v[j, d] for j in range(n_t)], axis=0)
-        acc = acc + mm_tn(block, nc_v[d])
-    gl_ref[...] = acc
-    collect_ten(2, st_v)
+        arrived(j != ten, st_v.at[j], st_r.at[j])
     summed = jnp.sum(st_v[...], axis=0)
     gg_ref[...] = summed[0:1, :wcol]
     glg_ref[...] = summed[0:1, wcol:]
@@ -603,7 +669,8 @@
     sine = jnp.asarray(np.sin(angle) * sign, F32)
     vm = pl.BlockSpec(memory_space=pltpu.VMEM)
     shape = jax.ShapeDtypeStruct
-    dma = pltpu.SemaphoreType.DMA
+    sem = lambda *dims: pltpu.SemaphoreType.DMA(dims)
+    small = wcol + ccol
     ig, gg, gq, gl, glg, ge, go = pl.pallas_call(
         lambda *refs: section_kernel((n_pipe, n, n_t, micros, seq), *refs),
         name="section_step",
@@ -620,45 +687,39 @@
         out_specs=(vm,) * 7,
         scratch_shapes=[
             pltpu.VMEM((rows, width), BF),
-            pltpu.VMEM((8, wcol + ccol), F32),
+            pltpu.VMEM((micros, seq, width), BF),
+            pltpu.VMEM((8, small), F32),
+            pltpu.VMEM((n, 8, small), F32),
+            pltpu.VMEM((share, width), BF),
             pltpu.VMEM((n_t, share, width), BF),
-            pltpu.VMEM((rows, width), BF),
+            pltpu.VMEM((share, width), BF),
             pltpu.VMEM((rows, n * ccol), BF),
-            pltpu.VMEM((n, 8, wcol + ccol), F32),
             pltpu.VMEM((n, wcol, qcols), BF),
-            pltpu.VMEM((n, 2, lcols // 2, wcol), BF),
+            pltpu.VMEM((n, n_t, lcols // n_t, wcol), BF),
             pltpu.VMEM((n, ccol, ecols), BF),
             pltpu.VMEM((n, orows, wcol), BF),
-            pltpu.VMEM((n, rows, wcol), BF),
-            pltpu.VMEM((n, rows, ccol), BF),
-            pltpu.VMEM((n, rows, orows), BF),
-            pltpu.VMEM((2, n, rows, wcol), BF),
-            pltpu.VMEM((n, rows, qcols), BF),
-            pltpu.VMEM((n, rows, ecols), BF),
-            pltpu.VMEM((n_t, n, share, lcols), BF),
+            pltpu.VMEM((n, n_t, share, wcol), BF),
+            pltpu.VMEM((n, n_t, share, ccol), BF),
+            pltpu.VMEM((n, n_t, share, wcol), BF),
+            pltpu.VMEM((n, n_t, share, lcols), BF),
+            pltpu.VMEM((rows, 5 * NOPE + orows), BF),
+            pltpu.VMEM((n, rows, 5 * NOPE + orows), BF),
+            pltpu.VMEM((rows, NOPE + orows), BF),
+            pltpu.VMEM((n, rows, NOPE + orows), BF),
             pltpu.VMEM((n_t, share, width), BF),
             pltpu.VMEM((n_t, share, width), BF),
             pltpu.VMEM((n_t, share, lcols), BF),
             pltpu.VMEM((n_t, share, lcols), BF),
-            pltpu.VMEM((rows, qcols), F32),
-            pltpu.VMEM((rows, lcols), F32),
             pltpu.VMEM((share, width), BF),
-            pltpu.VMEM((n, 8, wcol + ccol), F32),
-            pltpu.VMEM((n, 8, wcol + ccol), F32),
-            pltpu.VMEM((n_t, 8, wcol + ccol), F32),
-            dma((6,)),
-            dma((7, 2, n)),
-            dma((7, n)),
-            dma((n,)),
-            dma((n,)),
-            dma((6, n)),
-            dma((6, n)),
-            dma((4, n_t)),
-            dma((4, n_t)),
-            dma((n_t,)),
-            dma((n_t,)),
-            dma((n_t, n)),
-            dma((n_t, n)),
+            pltpu.VMEM((n, 8, small), F32),
+            pltpu.VMEM((n, 8, small), F32),
+            pltpu.VMEM((n_t, 8, small), F32),
+            pltpu.VMEM((n, rows, qcols), BF),
+            pltpu.VMEM((n, rows, ecols), BF),
+            sem(2, n), sem(2, n), sem(1), sem(1), sem(2, n), sem(n), sem(n, n_t), sem(n, n_t),
+            sem(3, n // 2), sem(3, n), sem(3, n), sem(3, n), sem(4, n), sem(4, n), sem(4, n, n_t), sem(4, n, n_t),
+            sem(2, n), sem(2, n), sem(2, n_t), sem(2, n_t), sem(n_t // 2 + 1), sem(n_t), sem(1), sem(n_t), sem(n_t),
+            sem(n_t), sem(n_t),
         ],
         compiler_params=pltpu.CompilerParams(
             collective_id=0, has_side_effects=True, vmem_limit_bytes=60 * 1024 * 1024
@@ -680,14 +741,19 @@
 
 def choose(saved, top_grad, gain, w_query, w_latent, compressed_gain, expand_weight, w_output):
     arrays = (saved, top_grad, gain, w_query, w_latent, compressed_gain, expand_weight, w_output)
-    n_t = lax.axis_size("tensor")
+    n, n_t = lax.axis_size("dp"), lax.axis_size("tensor")
     fits = (
-        lax.axis_size("dp") > 1
-        and n_t % 2 == 0
+        n % 2 == 0
+        and n_t == 4
+        and saved.shape[1] == 2
+        and saved.shape[2] == ROPE
         and w_query.shape[2] == 2 * (NOPE + ROPE)
+        and w_output.shape[1] == 2 * VDIM
         and gain.shape[1] % 128 == 0
         and compressed_gain.shape[1] % 128 == 0
-        and saved.shape[2] % (16 * n_t) == 0
+        and n * compressed_gain.shape[1] + ROPE == w_latent.shape[2]
+        and w_latent.shape[2] % (16 * n_t) == 0
+        and n <= 8
     )
     return section_step(*arrays) if fits else shards(*arrays)
 

time: 104 us -> 98 us (0.942)
  Pallas kernels: 103 us -> 97.2 us
    pallas_call x1, Pallas kernels: 101 us -> 94.7 us  [section_step(): pl.pallas_call(lambda *refs: section_kernel((n_pipe, n, n_t, micros, seq)...]
where the time goes in v1:
time: 98 us; the launch traced here: 97.9 us
  Pallas kernels  97.2 us (99%)
    pallas_call x1, Pallas kernels, section_step(): pl.pallas_call(lambda *refs: section_kernel((n_pipe, n, n_t, micros, seq)...  94.7 us
    pallas_call x1, Pallas kernels, section_step(): pl.pallas_call(hand_over, name='hand_over', out_shape=tuple((shape(p.shap...  2.54 us

profile of v1, /device:TPU:0, one launch (start us, length us, event | category | flops | bytes accessed | tf_op | source)
XLA Modules:
  0.0 97.9 jit_solution(8501300696454063968)
XLA Ops:
  0.6 94.7 %section_step.1 = (bf16[2,16,1024]{2,1,0:T(8,128)(2,1)}, f32[1,256]{1,0:T(1,128)}, f32[256,384]{1,0:T(8,128)}, f32[576,256]{1,0:T(8,128)}, f32[1,128]{1,0:T(1,12...) custom-call(bf16[2,64,1024]{2,1,0:T(8,128)(2,1)} %bitcast.15, bf16[2,64,1024]{2,1,0:T(8,128)(2,1)} %refs_1_.1, ...), custom_call_target="tpu_custom_call" | custom-call | tf_op jit(solution)/shard_map/section_step/pallas_call | solution.py:674
  95.3 2.5 %hand_over.1 = (bf16[2,16,1024]{2,1,0:T(8,128)(2,1)}, f32[1,256]{1,0:T(1,128)}, f32[256,384]{1,0:T(8,128)}, f32[576,256]{1,0:T(8,128)}, f32[1,128]{1,0:T(1,128)}...) custom-call(bf16[2,16,1024]{2,1,0:T(8,128)(2,1)} %get-tuple-element.21.refs_0_, f32[1,256]{1,0:T(1,128)} %get-tuple-element.22.refs_1_, ...), custom_call_target="tpu_custom_call" | custom-call | tf_op jit(solution)/shard_map/hand_over/pallas_call | solution.py:732

commit v2 on v1

--- a/solution.py
+++ b/solution.py
@@ -217,10 +217,10 @@
     saved_ref, top_ref, gain_ref, lgain_ref, wq_ref, wl_ref, we_ref, wo_ref, cos_ref, sin_ref,
     ig_ref, gg_ref, gq_ref, gl_ref, glg_ref, ge_ref, go_ref,
     x_v, xs_v, own_v, sm_v, nm_v, u_v, um_v, cb_v, wq_v, wl_v, we_v, wo_v,
-    nc_v, cc_v, uc_v, dl_v, fo_v, fw_v, so_v, sv_v, part_v, rs_v, lp_v, ls_v, dx_v, sg_v, sr_v, st_v,
+    nc_v, cc_v, uc_v, dl_v, rk_v, ro_v, fo_v, fw_v, so_v, sv_v, part_v, rs_v, lp_v, ls_v, dx_v, sg_v, sr_v, st_v,
     dq_v, de_v,
-    dp_s, dp_r, x_s, x_r, line_s, line_r, wt_s, wt_r, w_s, w_r, f_s, f_r, z_s, z_r, t_s, t_r,
-    b_s, b_r, rs_s, rs_r, p_s, u_r, um_r, uf_s, uf_r, st_s, st_r,
+    dp_s, dp_r, x_s, x_r, wz_s, wz_r, wh_s, wt_s, wt_r, w_s, w_r, f_s, f_r, z_s, z_r, t_s, t_r,
+    b_s, b_r, bh_s, rs_s, rs_r, p_s, u_r, um_r, uf_s, uf_r, st_s, st_r,
 ):
     n_pipe, n, n_t, micros, seq = dims
     sec, me, ten = lax.axis_index("pipe"), lax.axis_index("dp"), lax.axis_index("tensor")
@@ -239,6 +239,9 @@
     block = me - par + core
     primary = core == par
     secondary = jnp.logical_not(primary)
+    half = me // 2
+    near = 2 - half
+    middle = jnp.logical_or(me == 1, me == 2)
     last = sec == n_pipe - 1
     lower = jnp.logical_not(last)
     both = jnp.logical_and
@@ -326,13 +329,14 @@
                 cond = both(cond, gate)
             begin(cond, rcopy(source(e), dest.at[slot, rank_to], z_s.at[k, e], z_r.at[k, slot], dev(e, rank_to)))
 
-    def relay(k, dest, owned=None):
+    def relay(k, dest, owned=None, gate=None):
         for b in range(n):
             here = b == me if owned is None else both(b == me, owned)
-            arrived(jnp.logical_not(here), dest.at[b, ten], z_r.at[k, b])
+            away = jnp.logical_not(here)
+            arrived(away if gate is None else both(away, gate), dest.at[b, ten], z_r.at[k, b])
             for j in range(n_t):
                 begin(
-                    j != ten,
+                    j != ten if gate is None else both(j != ten, gate),
                     rcopy(dest.at[b, ten], dest.at[b, ten], t_s.at[k, b, j], t_r.at[k, b, ten], dev(me, j)),
                 )
 
@@ -343,51 +347,42 @@
 
     def spread_block(k, source, dest, gate=None):
         for e in range(n):
-            cond = jnp.logical_or(e != me, secondary)
+            cond = both(jnp.logical_or(e != me, secondary), jnp.logical_or(half == e // 2, near == e))
             if gate is not None:
                 cond = both(cond, gate)
             begin(cond, rcopy(source, dest.at[block], b_s.at[k, e], b_r.at[k, block], dev(e, group)))
 
+    def hand_on(k, dest, gate=None):
+        for b in range(n):
+            cond = both(middle, half != b // 2)
+            if gate is not None:
+                cond = both(cond, gate)
+            arrived(cond, dest.at[b], b_r.at[k, b])
+            begin(cond, rcopy(dest.at[b], dest.at[b], bh_s.at[k, b], b_r.at[k, b], dev(mate, ten)))
+
     def collect_block(k, dest):
         for b in range(n):
-            arrived(jnp.logical_or(b != me, secondary), dest.at[b], b_r.at[k, b])
-
-    def line_start(source, at):
-        begin(me < n - 1, rcopy(source, at(me), line_s.at[0, 0], line_r.at[me], dev(me + 1, ten)))
-        begin(me > 0, rcopy(source, at(me), line_s.at[1, 0], line_r.at[me], dev(me - 1, ten)))
-
-    def line_step(at, s, extra):
-        for way, b, valid, more, dest in (
-            (0, jnp.maximum(me - 1 - s, 0), me - 1 - s >= 0, me < n - 1, me + 1),
-            (1, jnp.minimum(me + 1 + s, n - 1), me + 1 + s <= n - 1, me > 0, me - 1),
-        ):
-            copy = rcopy(at(b), at(b), line_s.at[way, s + 1], line_r.at[b], dev(dest, ten))
-
-            @pl.when(valid)
-            def _():
-                copy.wait_recv()
-
-            if s < n - 2:
-                begin(both(valid, more), copy)
-            extra(b, valid)
+            handed = both(middle, half != b // 2)
+            cond = both(jnp.logical_or(b != me, secondary), jnp.logical_not(handed))
+            arrived(cond, dest.at[b], b_r.at[k, b])
 
     spread_dp(0, lambda j: own_v, sm_v)
     sm_v[me] = own_v[...]
     begin(primary, rcopy(saved_ref, xs_v, x_s.at[0], x_r.at[0], dev(mate, ten)))
-    line_start(
-        wl_ref.at[pl.ds(pl.multiple_of(ten * quarter, quarter), quarter)], lambda b: wl_v.at[b, ten]
-    )
+    my_quarter = wl_ref.at[pl.ds(pl.multiple_of(ten * quarter, quarter), quarter)]
+    for i, level in enumerate((near, mate)):
+        begin(me >= 0, rcopy(my_quarter, wl_v.at[me, ten], wz_s.at[i], wz_r.at[me], dev(level, ten)))
     weights = ((wq_ref, wq_v), (we_ref, we_v), (wo_ref, wo_v))
-    for k, (ref, store) in enumerate(weights):
+
+    def give(k):
+        ref, store = weights[k]
         for i in range(n // 2):
             level = 2 * i + core
             begin(level != me, rcopy(ref, store.at[me], w_s.at[k, i], w_r.at[k, me], dev(level, ten)))
         begin(primary, rcopy(ref, store.at[me], f_s.at[k, me], f_r.at[k, me], dev(me, partner)))
-    for s in range(n_t):
-        begin(both(last, primary), rcopy(u_v.at[s], u_v.at[s], uf_s.at[s], uf_r.at[s], dev(mate, ten)))
+
+    give(0)
     um_cols = lambda e: um_v.at[:, pl.ds(e * wcol, wcol)]
-    spread_z(2, um_cols, uc_v, me, ten, gate=last)
-
     for j in range(n_t):
         wl_v[me, j] = wl_ref[j * quarter : (j + 1) * quarter]
 
@@ -410,21 +405,34 @@
         def _():
             nc_v[j, ten] = nm_v[:, cols(j, wcol)]
 
-    @pl.when(secondary)
-    def _():
-        rcopy(xs_v, xs_v, x_s.at[0], x_r.at[0], dev(me, partner)).wait_recv()
-        by_share(x_store, xs_v)
-
-    x32 = x_v[...].astype(F32)
-    r = lax.rsqrt(jnp.mean(x32 * x32, axis=1, keepdims=True) + EPS)
-    nb = (x32 * r * gain).astype(BF)
-
     def to_ten(b, valid):
         for j in range(n_t):
             begin(
                 both(valid, j != ten),
                 rcopy(wl_v.at[b, ten], wl_v.at[b, ten], wt_s.at[b, j], wt_r.at[b, ten], dev(me, j)),
             )
+
+    for b in range(n):
+        arrived(b != me, wl_v.at[b, ten], wz_r.at[b])
+        begin(
+            both(middle, half != b // 2),
+            rcopy(wl_v.at[b, ten], wl_v.at[b, ten], wh_s.at[b], wz_r.at[b], dev(mate, ten)),
+        )
+        to_ten(b, b != me)
+    give(1)
+    give(2)
+    for s in range(n_t):
+        begin(both(last, primary), rcopy(u_v.at[s], u_v.at[s], uf_s.at[s], uf_r.at[s], dev(mate, ten)))
+    spread_z(2, um_cols, uc_v, me, ten, gate=last)
+
+    @pl.when(secondary)
+    def _():
+        rcopy(xs_v, xs_v, x_s.at[0], x_r.at[0], dev(me, partner)).wait_recv()
+        by_share(x_store, xs_v)
+
+    x32 = x_v[...].astype(F32)
+    r = lax.rsqrt(jnp.mean(x32 * x32, axis=1, keepdims=True) + EPS)
+    nb = (x32 * r * gain).astype(BF)
 
     def take(k):
         store = weights[k][1]
@@ -435,8 +443,6 @@
         for d in range(n):
             arrived(secondary, store.at[d], f_r.at[k, d])
 
-    for s in range(n - 1):
-        line_step(lambda b: wl_v.at[b, ten], s, to_ten)
     take(0)
     for d in range(n):
         for j in range(n_t):
@@ -463,6 +469,14 @@
     lr = lat[:, rank:]
     lr2 = jnp.concatenate([lr, lr], axis=1)
     rk = (lr2 * cosine + half_swap(lr2) * sine).astype(BF)
+    ro_v[...] = rk
+    spread_z(4, lambda e: ro_v.at[my_rows], rk_v, block, group)
+
+    @pl.when(primary)
+    def _():
+        rk_v[me, ten] = ro_v[my_rows]
+
+    relay(0, nc_v)
     lane = lax.broadcasted_iota(jnp.int32, (rows, 2 * ROPE), 1)
     low = lane < ROPE
     q1, q2 = q[:, NOPE : 2 * NOPE], q[:, 2 * NOPE :]
@@ -496,9 +510,8 @@
         wb = w32.astype(BF)
         fo_v[:, cols(h, NOPE)] = qn
         fo_v[:, cols(2 + h, NOPE)] = kn
-        fo_v[:, cols(5 + h, VDIM)] = mm(wb, vv).astype(BF)
+        fo_v[:, cols(4 + h, VDIM)] = mm(wb, vv).astype(BF)
         heads.append((qn, kn, vv, qh, w32, wb))
-    fo_v[:, cols(4, NOPE)] = rk
 
     @pl.when(primary)
     def _():
@@ -506,6 +519,9 @@
 
     spread_block(0, fo_v, fw_v, gate=lower)
     take(2)
+    relay(1, cc_v, owned=primary, gate=lower)
+    relay(4, rk_v, owned=primary, gate=lower)
+    hand_on(0, fw_v, gate=lower)
 
     for s in range(n_t):
         cond = both(lower, primary)
@@ -582,8 +598,6 @@
         sv_v[me] = so_v[...]
 
     spread_block(1, so_v, sv_v, gate=lower)
-    relay(0, nc_v)
-    relay(1, cc_v, owned=primary)
 
     def collect_shares(k, dest):
         for g in range(n_t):
@@ -612,19 +626,24 @@
     spread_block(0, fo_v, fw_v, gate=last)
     for m in range(micros):
         ig_ref[m] = dx[m * chunk : (m + 1) * chunk].astype(BF)
+    relay(1, cc_v, owned=primary, gate=last)
+    relay(4, rk_v, owned=primary, gate=last)
     relay(2, uc_v)
+    hand_on(1, sv_v)
     relay(3, dl_v)
+    hand_on(0, fw_v, gate=last)
     collect_dp(1, sr_v)
     st_v[ten] = jnp.sum(sr_v[...], axis=0)
     for j in range(n_t):
         begin(j != ten, rcopy(st_v.at[ten], st_v.at[ten], st_s.at[j], st_r.at[ten], dev(me, j)))
     collect_block(0, fw_v)
     collect_block(1, sv_v)
+    collect(4, rk_v)
     for b in range(n):
         few = sv_v[b, :, :NOPE]
         ds = [jnp.where(same, mm_nt(few, picks[h]), 0.0).astype(BF) for h in range(2)]
         part = lambda i: fw_v[b, :, cols(i, NOPE)]
-        dq_v[b] = query_grad(ds, part(2), part(3), part(4))
+        dq_v[b] = query_grad(ds, part(2), part(3), rk_v[b].reshape(rows, 2 * ROPE))
         for h in range(2):
             de_v[b, :, cols(2 * h, NOPE)] = mm_tn(ds[h], part(h)).astype(BF)
             de_v[b, :, cols(2 * h + 1, NOPE)] = sv_v[b, :, cols(1 + h, VDIM)]
@@ -633,7 +652,7 @@
     gq_ref[...] = mm_tn(nc_v[...].reshape(n * rows, wcol), dq_v[...].reshape(n * rows, dq_v.shape[2]))
     ge_ref[...] = mm_tn(cc_v[...].reshape(n * rows, ccol), de_v[...].reshape(n * rows, de_v.shape[2]))
     collect(2, uc_v)
-    mixed = fw_v[:, :, 5 * NOPE :].reshape(n * rows, 2 * VDIM)
+    mixed = fw_v[:, :, 4 * NOPE :].reshape(n * rows, 2 * VDIM)
     go_ref[...] = mm_tn(mixed, uc_v[...].reshape(n * rows, wcol))
     collect(3, dl_v)
     gl_ref[...] = mm_tn(dl_v[...].reshape(n * rows, dl_v.shape[3]), nc_v[...].reshape(n * rows, wcol))
@@ -669,19 +688,20 @@
     sine = jnp.asarray(np.sin(angle) * sign, F32)
     vm = pl.BlockSpec(memory_space=pltpu.VMEM)
     shape = jax.ShapeDtypeStruct
+    kept = pltpu.VMEM
     sem = lambda *dims: pltpu.SemaphoreType.DMA(dims)
     small = wcol + ccol
     ig, gg, gq, gl, glg, ge, go = pl.pallas_call(
         lambda *refs: section_kernel((n_pipe, n, n_t, micros, seq), *refs),
         name="section_step",
         out_shape=(
-            shape((micros, seq // n_t, width), BF),
-            shape((1, wcol), F32),
-            shape((wcol, qcols), F32),
-            shape((lcols, wcol), F32),
-            shape((1, ccol), F32),
-            shape((ccol, ecols), F32),
-            shape((orows, wcol), F32),
+            kept((micros, seq // n_t, width), BF),
+            kept((1, wcol), F32),
+            kept((wcol, qcols), F32),
+            kept((lcols, wcol), F32),
+            kept((1, ccol), F32),
+            kept((ccol, ecols), F32),
+            kept((orows, wcol), F32),
         ),
         in_specs=[vm] * 10,
         out_specs=(vm,) * 7,
@@ -702,8 +722,10 @@
             pltpu.VMEM((n, n_t, share, ccol), BF),
             pltpu.VMEM((n, n_t, share, wcol), BF),
             pltpu.VMEM((n, n_t, share, lcols), BF),
-            pltpu.VMEM((rows, 5 * NOPE + orows), BF),
-            pltpu.VMEM((n, rows, 5 * NOPE + orows), BF),
+            pltpu.VMEM((n, n_t, share, 2 * ROPE), BF),
+            pltpu.VMEM((rows, 2 * ROPE), BF),
+            pltpu.VMEM((rows, 4 * NOPE + orows), BF),
+            pltpu.VMEM((n, rows, 4 * NOPE + orows), BF),
             pltpu.VMEM((rows, NOPE + orows), BF),
             pltpu.VMEM((n, rows, NOPE + orows), BF),
             pltpu.VMEM((n_t, share, width), BF),
@@ -716,9 +738,9 @@
             pltpu.VMEM((n_t, 8, small), F32),
             pltpu.VMEM((n, rows, qcols), BF),
             pltpu.VMEM((n, rows, ecols), BF),
-            sem(2, n), sem(2, n), sem(1), sem(1), sem(2, n), sem(n), sem(n, n_t), sem(n, n_t),
-            sem(3, n // 2), sem(3, n), sem(3, n), sem(3, n), sem(4, n), sem(4, n), sem(4, n, n_t), sem(4, n, n_t),
-            sem(2, n), sem(2, n), sem(2, n_t), sem(2, n_t), sem(n_t // 2 + 1), sem(n_t), sem(1), sem(n_t), sem(n_t),
+            sem(2, n), sem(2, n), sem(1), sem(1), sem(2), sem(n), sem(n), sem(n, n_t), sem(n, n_t),
+            sem(3, n // 2), sem(3, n), sem(3, n), sem(3, n), sem(5, n), sem(5, n), sem(5, n, n_t), sem(5, n, n_t),
+            sem(2, n), sem(2, n), sem(2, n), sem(2, n_t), sem(2, n_t), sem(n_t // 2 + 1), sem(n_t), sem(1), sem(n_t), sem(n_t),
             sem(n_t), sem(n_t),
         ],
         compiler_params=pltpu.CompilerParams(
@@ -728,7 +750,7 @@
         saved[0], top_grad, gain, compressed_gain, w_query[0], w_latent[0].T,
         expand_weight[0], w_output[0], cosine, sine,
     )
-    parts = (ig, gg, gq, gl, glg, ge, go)
+    parts = [pltpu.with_memory_space_constraint(p, pltpu.VMEM) for p in (ig, gg, gq, gl, glg, ge, go)]
     ig, gg, gq, gl, glg, ge, go = pl.pallas_call(
         hand_over,
         name="hand_over",
@@ -743,7 +765,7 @@
     arrays = (saved, top_grad, gain, w_query, w_latent, compressed_gain, expand_weight, w_output)
     n, n_t = lax.axis_size("dp"), lax.axis_size("tensor")
     fits = (
-        n % 2 == 0
+        n == 4
         and n_t == 4
         and saved.shape[1] == 2
         and saved.shape[2] == ROPE
@@ -753,7 +775,6 @@
         and compressed_gain.shape[1] % 128 == 0
         and n * compressed_gain.shape[1] + ROPE == w_latent.shape[2]
         and w_latent.shape[2] % (16 * n_t) == 0
-        and n <= 8
     )
     return section_step(*arrays) if fits else shards(*arrays)
 

time: 98 us -> 84.5 us (0.86); the launches traced: 97.9 us -> 83 us
  Pallas kernels: 97.2 us -> 82.3 us
    pallas_call x1, Pallas kernels: 94.7 us -> 81.1 us  [section_step(): pl.pallas_call(lambda *refs: section_kernel((n_pipe, n, n_t, micros, seq)...]
    pallas_call x1, Pallas kernels: 2.54 us -> 1.24 us  [section_step(): pl.pallas_call(hand_over, name='hand_over', out_shape=tuple((shape(p.shap...]
where the time goes in v2:
time: 84.5 us; the launch traced here: 83 us
  Pallas kernels  82.3 us (97%)
    pallas_call x1, Pallas kernels, section_step(): pl.pallas_call(lambda *refs: section_kernel((n_pipe, n, n_t, micros, seq)...  81.1 us

profile of v2, /device:TPU:0, one launch (start us, length us, event | category | flops | bytes accessed | tf_op | source)
XLA Modules:
  0.0 83.0 jit_solution(10278179425003636728)
XLA Ops:
  0.6 81.1 %section_step.1 = (bf16[2,16,1024]{2,1,0:T(8,128)(2,1)S(1)}, f32[1,256]{1,0:T(1,128)S(1)}, f32[256,384]{1,0:T(8,128)S(1)}, f32[576,256]{1,0:T(8,128)S(1)}, f32[1...) custom-call(bf16[2,64,1024]{2,1,0:T(8,128)(2,1)} %bitcast.15, bf16[2,64,1024]{2,1,0:T(8,128)(2,1)} %refs_1_.1, ...), custom_call_target="tpu_custom_call" | custom-call | tf_op jit(solution)/shard_map/section_step/pallas_call | solution.py:694
  81.7 1.2 %hand_over.1 = (bf16[2,16,1024]{2,1,0:T(8,128)(2,1)}, f32[1,256]{1,0:T(1,128)}, f32[256,384]{1,0:T(8,128)}, f32[576,256]{1,0:T(8,128)}, f32[1,128]{1,0:T(1,128)}...) custom-call(bf16[2,16,1024]{2,1,0:T(8,128)(2,1)S(1)} %get-tuple-element.21.refs_0_, f32[1,256]{1,0:T(1,128)S(1)} %get-tuple-element.22.refs_1_, ...), custom_call_target="tpu_custom_call" | custom-call | tf_op jit(solution)/shard_map/hand_over/pallas_call | solution.py:754

commit v3 on v2

--- a/solution.py
+++ b/solution.py
@@ -217,10 +217,10 @@
     saved_ref, top_ref, gain_ref, lgain_ref, wq_ref, wl_ref, we_ref, wo_ref, cos_ref, sin_ref,
     ig_ref, gg_ref, gq_ref, gl_ref, glg_ref, ge_ref, go_ref,
     x_v, xs_v, own_v, sm_v, nm_v, u_v, um_v, cb_v, wq_v, wl_v, we_v, wo_v,
-    nc_v, cc_v, uc_v, dl_v, rk_v, ro_v, fo_v, fw_v, so_v, sv_v, part_v, rs_v, lp_v, ls_v, dx_v, sg_v, sr_v, st_v,
+    nc_v, cc_v, uc_v, dl_v, rk_v, ro_v, fo_v, fw_v, so_v, sv_v, part_v, rs_v, lp_v, ls_v, dx_v, sg_v, sr_v,
     dq_v, de_v,
-    dp_s, dp_r, x_s, x_r, wz_s, wz_r, wh_s, wt_s, wt_r, w_s, w_r, f_s, f_r, z_s, z_r, t_s, t_r,
-    b_s, b_r, bh_s, rs_s, rs_r, p_s, u_r, um_r, uf_s, uf_r, st_s, st_r,
+    dp_s, dp_r, x_s, x_r, wz_s, wz_r, wh_s, wt_s, wt_r, w_s, w_r, f_s, f_r, z_s, z_r, zl_r, t_s, ta_r, tb_r,
+    b_s, b_r, bh_s, rs_s, rs_r, p_s, u_r, um_r, uf_s, uf_r, sg_s, sg_r,
 ):
     n_pipe, n, n_t, micros, seq = dims
     sec, me, ten = lax.axis_index("pipe"), lax.axis_index("dp"), lax.axis_index("tensor")
@@ -233,6 +233,7 @@
     quarter = wl_v.shape[2]
     core = lax.rem(ten, 2)
     partner = ten + 1 - 2 * core
+    opposite = lax.rem(ten + 2, n_t)
     par = lax.rem(me, 2)
     mate = me + 1 - 2 * par
     group = ten - core + par
@@ -252,12 +253,16 @@
             src_ref=a, dst_ref=b, send_sem=ss, recv_sem=rs, device_id=dev, device_id_type=MESH
         )
 
-    def begin(cond, copy):
+    def begin(cond, copy, sent=False):
         @pl.when(cond)
         def _():
             copy.start()
 
-        drains.append((cond, copy))
+        if not sent:
+            drains.append((cond, copy))
+
+    def settle(cond, ref, ss):
+        drains.append((cond, rcopy(ref, ref, ss, x_r.at[0], dev(me, partner))))
 
     def arrived(cond, ref, rs):
         @pl.when(cond)
@@ -316,73 +321,118 @@
 
     def spread_dp(k, source, dest):
         for j in range(n):
-            begin(j != me, rcopy(source(j), dest.at[me], dp_s.at[k, j], dp_r.at[k, me], dev(j, ten)))
+            begin(j != me, rcopy(source(j), dest.at[me], dp_s.at[k], dp_r.at[k], dev(j, ten)), sent=True)
+        settle(me >= 0, dest.at[pl.ds(0, n - 1)], dp_s.at[k])
 
     def collect_dp(k, dest):
-        for j in range(n):
-            arrived(j != me, dest.at[j], dp_r.at[k, j])
+        arrived(me >= 0, dest.at[pl.ds(0, n - 1)], dp_r.at[k])
 
     def spread_z(k, source, dest, slot, rank_to, gate=None):
         for e in range(n):
             cond = jnp.logical_or(e != me, rank_to != ten)
             if gate is not None:
                 cond = both(cond, gate)
-            begin(cond, rcopy(source(e), dest.at[slot, rank_to], z_s.at[k, e], z_r.at[k, slot], dev(e, rank_to)))
-
-    def relay(k, dest, owned=None, gate=None):
+            rs = zl_r.at[slot] if k == 3 else z_r.at[k]
+            begin(cond, rcopy(source(e), dest.at[slot, rank_to], z_s.at[k], rs, dev(e, rank_to)), sent=True)
+        on = me >= 0 if gate is None else gate
+        if k in (1, 4):
+            settle(both(on, primary), dest.at[0, pl.ds(0, n - 1)], z_s.at[k])
+            settle(both(on, secondary), dest.at[0, pl.ds(0, n)], z_s.at[k])
+        else:
+            settle(on, dest.at[0, pl.ds(0, n - 1)], z_s.at[k])
+
+    def relay(k, dest, gate):
+        def share_slot(b):
+            for to, rs in ((opposite, ta_r), (partner, tb_r)):
+                copy = rcopy(dest.at[b, ten], dest.at[b, ten], t_s.at[k], rs.at[k], dev(me, to))
+                begin(gate, copy, sent=True)
+
+        if k == 3:
+            for b in range(n):
+                arrived(both(b != me, gate), dest.at[b, ten], zl_r.at[b])
+                share_slot(b)
+        else:
+            few, every = dest.at[pl.ds(0, n - 1), ten], dest.at[pl.ds(0, n), ten]
+            if k in (1, 4):
+                arrived(both(gate, primary), few, z_r.at[k])
+                arrived(both(gate, secondary), every, z_r.at[k])
+            else:
+                arrived(gate, few, z_r.at[k])
+            for b in range(n):
+                share_slot(b)
+
+    def pass_on(k, dest):
+        arrived(me >= 0, dest.at[pl.ds(0, n), opposite], ta_r.at[k])
         for b in range(n):
-            here = b == me if owned is None else both(b == me, owned)
-            away = jnp.logical_not(here)
-            arrived(away if gate is None else both(away, gate), dest.at[b, ten], z_r.at[k, b])
-            for j in range(n_t):
-                begin(
-                    j != ten if gate is None else both(j != ten, gate),
-                    rcopy(dest.at[b, ten], dest.at[b, ten], t_s.at[k, b, j], t_r.at[k, b, ten], dev(me, j)),
-                )
+            at = dest.at[b, opposite]
+            begin(me >= 0, rcopy(at, at, t_s.at[k], tb_r.at[k], dev(me, partner)), sent=True)
+        settle(me >= 0, dest.at[pl.ds(0, n - 1)], t_s.at[k])
 
     def collect(k, dest):
+        arrived(me >= 0, dest.at[pl.ds(0, 2)], tb_r.at[k])
+
+    def landing(k, b):
+        return sv_v.at[b] if k == 3 else fw_v.at[b, k]
+
+    def spread_block(k, gate, across):
+        source = so_v if k == 3 else fo_v.at[k]
+        for e in range(n):
+            wanted = near == e if across else both(half == e // 2, jnp.logical_or(e != me, secondary))
+            copy = rcopy(source, landing(k, block), b_s.at[k], b_r.at[k, block], dev(e, group))
+            begin(both(wanted, gate), copy, sent=True)
+        if across:
+            several = lambda c: sv_v.at[pl.ds(0, c)] if k == 3 else fw_v.at[pl.ds(0, c), k]
+            settle(both(gate, primary), several(2), b_s.at[k])
+            settle(both(gate, secondary), several(3), b_s.at[k])
+
+    def hand_on(k, gate):
         for b in range(n):
-            for j in range(n_t):
-                arrived(j != ten, dest.at[b, j], t_r.at[k, b, j])
-
-    def spread_block(k, source, dest, gate=None):
-        for e in range(n):
-            cond = both(jnp.logical_or(e != me, secondary), jnp.logical_or(half == e // 2, near == e))
-            if gate is not None:
-                cond = both(cond, gate)
-            begin(cond, rcopy(source, dest.at[block], b_s.at[k, e], b_r.at[k, block], dev(e, group)))
-
-    def hand_on(k, dest, gate=None):
-        for b in range(n):
-            cond = both(middle, half != b // 2)
-            if gate is not None:
-                cond = both(cond, gate)
-            arrived(cond, dest.at[b], b_r.at[k, b])
-            begin(cond, rcopy(dest.at[b], dest.at[b], bh_s.at[k, b], b_r.at[k, b], dev(mate, ten)))
-
-    def collect_block(k, dest):
+            cond = both(both(middle, half != b // 2), gate)
+            at = landing(k, b)
+            arrived(cond, at, b_r.at[k, b])
+            begin(cond, rcopy(at, at, bh_s.at[k], b_r.at[k, b], dev(mate, ten)), sent=True)
+        two = sv_v.at[pl.ds(0, 2)] if k == 3 else fw_v.at[pl.ds(0, 2), k]
+        settle(both(middle, gate), two, bh_s.at[k])
+
+    def collect_block(k):
         for b in range(n):
             handed = both(middle, half != b // 2)
             cond = both(jnp.logical_or(b != me, secondary), jnp.logical_not(handed))
-            arrived(cond, dest.at[b], b_r.at[k, b])
+            arrived(cond, landing(k, b), b_r.at[k, b])
 
     spread_dp(0, lambda j: own_v, sm_v)
     sm_v[me] = own_v[...]
+    my_quarter = wl_ref.at[pl.ds(pl.multiple_of(ten * quarter, quarter), quarter)]
+    for level in (near, mate):
+        begin(me >= 0, rcopy(my_quarter, wl_v.at[me, ten], wz_s.at[0], wz_r.at[me], dev(level, ten)), sent=True)
+    settle(me >= 0, wl_v.at[0, pl.ds(0, 2)], wz_s.at[0])
+    weights = ((wq_ref, wq_v), (we_ref, we_v), (wo_ref, wo_v))
+
     begin(primary, rcopy(saved_ref, xs_v, x_s.at[0], x_r.at[0], dev(mate, ten)))
-    my_quarter = wl_ref.at[pl.ds(pl.multiple_of(ten * quarter, quarter), quarter)]
-    for i, level in enumerate((near, mate)):
-        begin(me >= 0, rcopy(my_quarter, wl_v.at[me, ten], wz_s.at[i], wz_r.at[me], dev(level, ten)))
-    weights = ((wq_ref, wq_v), (we_ref, we_v), (wo_ref, wo_v))
-
-    def give(k):
+
+    def give(k, gate=True):
         ref, store = weights[k]
         for i in range(n // 2):
             level = 2 * i + core
-            begin(level != me, rcopy(ref, store.at[me], w_s.at[k, i], w_r.at[k, me], dev(level, ten)))
-        begin(primary, rcopy(ref, store.at[me], f_s.at[k, me], f_r.at[k, me], dev(me, partner)))
-
+            copy = rcopy(ref, store.at[me], w_s.at[k], w_r.at[k, me], dev(level, ten))
+            begin(both(level != me, gate), copy, sent=True)
+        settle(both(primary, gate), store.at[pl.ds(0, n // 2 - 1)], w_s.at[k])
+        settle(both(secondary, gate), store.at[pl.ds(0, n // 2)], w_s.at[k])
+        copy = rcopy(ref, store.at[me], f_s.at[k], f_r.at[k], dev(me, partner))
+        begin(both(primary, gate), copy, sent=True)
+
+    def give_rest(gate):
+        give(1, gate)
+        for s in range(n_t):
+            copy = rcopy(u_v.at[s], u_v.at[s], uf_s.at[0], uf_r.at[0], dev(mate, ten))
+            begin(both(both(last, primary), gate), copy, sent=True)
+        give(2, gate)
+        spread_z(2, um_cols, uc_v, me, ten, gate=both(last, gate))
+
+    um_cols = lambda e: um_v.at[:, pl.ds(e * wcol, wcol)]
     give(0)
-    um_cols = lambda e: um_v.at[:, pl.ds(e * wcol, wcol)]
+    give_rest(jnp.logical_not(middle))
+
     for j in range(n_t):
         wl_v[me, j] = wl_ref[j * quarter : (j + 1) * quarter]
 
@@ -392,6 +442,27 @@
             store[me] = ref[...]
 
         by_share(x_store, saved_ref)
+
+    def to_ten(b, valid):
+        for j in range(n_t):
+            begin(
+                both(valid, j != ten),
+                rcopy(wl_v.at[b, ten], wl_v.at[b, ten], wt_s.at[0], wt_r.at[0], dev(me, j)),
+                sent=True,
+            )
+
+    for b in range(n):
+        arrived(b != me, wl_v.at[b, ten], wz_r.at[b])
+        begin(
+            both(middle, half != b // 2),
+            rcopy(wl_v.at[b, ten], wl_v.at[b, ten], wh_s.at[0], wz_r.at[b], dev(mate, ten)),
+            sent=True,
+        )
+        to_ten(b, b != me)
+    settle(middle, wl_v.at[0, pl.ds(0, 2)], wh_s.at[0])
+    wl_peers = wl_v.at[pl.ds(0, n - 1), pl.ds(0, n_t - 1)]
+    settle(me >= 0, wl_peers, wt_s.at[0])
+    give_rest(middle)
 
     collect_dp(0, sm_v)
     gain = jnp.concatenate([sm_v[d][0:1, :wcol] for d in range(n)], axis=1)
@@ -405,26 +476,6 @@
         def _():
             nc_v[j, ten] = nm_v[:, cols(j, wcol)]
 
-    def to_ten(b, valid):
-        for j in range(n_t):
-            begin(
-                both(valid, j != ten),
-                rcopy(wl_v.at[b, ten], wl_v.at[b, ten], wt_s.at[b, j], wt_r.at[b, ten], dev(me, j)),
-            )
-
-    for b in range(n):
-        arrived(b != me, wl_v.at[b, ten], wz_r.at[b])
-        begin(
-            both(middle, half != b // 2),
-            rcopy(wl_v.at[b, ten], wl_v.at[b, ten], wh_s.at[b], wz_r.at[b], dev(mate, ten)),
-        )
-        to_ten(b, b != me)
-    give(1)
-    give(2)
-    for s in range(n_t):
-        begin(both(last, primary), rcopy(u_v.at[s], u_v.at[s], uf_s.at[s], uf_r.at[s], dev(mate, ten)))
-    spread_z(2, um_cols, uc_v, me, ten, gate=last)
-
     @pl.when(secondary)
     def _():
         rcopy(xs_v, xs_v, x_s.at[0], x_r.at[0], dev(me, partner)).wait_recv()
@@ -439,14 +490,12 @@
         for d in range(n):
             cond = both(primary, d != me)
             arrived(cond, store.at[d], w_r.at[k, d])
-            begin(cond, rcopy(store.at[d], store.at[d], f_s.at[k, d], f_r.at[k, d], dev(me, partner)))
-        for d in range(n):
-            arrived(secondary, store.at[d], f_r.at[k, d])
+            begin(cond, rcopy(store.at[d], store.at[d], f_s.at[k], f_r.at[k], dev(me, partner)), sent=True)
+        settle(primary, store, f_s.at[k])
+        arrived(secondary, store, f_r.at[k])
 
     take(0)
-    for d in range(n):
-        for j in range(n_t):
-            arrived(both(d != me, j != ten), wl_v.at[d, j], wt_r.at[d, j])
+    arrived(me >= 0, wl_peers, wt_r.at[0])
 
     wq = wq_v[...].reshape(width, wq_v.shape[2])
     wl = [wl_v[d].reshape(n_t * quarter, wcol) for d in range(n)]
@@ -476,11 +525,14 @@
     def _():
         rk_v[me, ten] = ro_v[my_rows]
 
-    relay(0, nc_v)
     lane = lax.broadcasted_iota(jnp.int32, (rows, 2 * ROPE), 1)
     low = lane < ROPE
     q1, q2 = q[:, NOPE : 2 * NOPE], q[:, 2 * NOPE :]
     nope = (q[:, :NOPE], pltpu.roll(jnp.where(low, q2, q1), ROPE, 1))
+    for h in range(2):
+        fo_v[0, :, cols(h, NOPE)] = nope[h].astype(BF)
+    spread_block(0, lower, True)
+    spread_block(0, lower, False)
     qr_all = jnp.where(low, q1, q2)
     qr = qr_all * cosine + half_swap(qr_all) * sine
     row = lax.broadcasted_iota(jnp.int32, (rows, rows), 0)
@@ -497,6 +549,10 @@
     take(1)
     we = we_v[...].reshape(n * ccol, we_v.shape[2])
     ex = mm(cb, we)
+    for h in range(2):
+        fo_v[1, :, cols(h, NOPE)] = ex[:, cols(2 * h, NOPE)].astype(BF)
+    spread_block(1, lower, True)
+    spread_block(1, lower, False)
     heads = []
     for h in range(2):
         qn = nope[h].astype(BF)
@@ -508,25 +564,27 @@
         e = jnp.exp(scores - jnp.max(scores, axis=1, keepdims=True))
         w32 = e / jnp.sum(e, axis=1, keepdims=True)
         wb = w32.astype(BF)
-        fo_v[:, cols(h, NOPE)] = qn
-        fo_v[:, cols(2 + h, NOPE)] = kn
-        fo_v[:, cols(4 + h, VDIM)] = mm(wb, vv).astype(BF)
+        fo_v[2, :, cols(h, VDIM)] = mm(wb, vv).astype(BF)
         heads.append((qn, kn, vv, qh, w32, wb))
 
     @pl.when(primary)
     def _():
         fw_v[me] = fo_v[...]
 
-    spread_block(0, fo_v, fw_v, gate=lower)
+    spread_block(2, lower, True)
+    spread_block(2, lower, False)
     take(2)
-    relay(1, cc_v, owned=primary, gate=lower)
-    relay(4, rk_v, owned=primary, gate=lower)
-    hand_on(0, fw_v, gate=lower)
+    relay(0, nc_v, gate=lower)
+    relay(1, cc_v, gate=lower)
+    relay(4, rk_v, gate=lower)
+    for k in range(3):
+        hand_on(k, lower)
 
     for s in range(n_t):
         cond = both(lower, primary)
         arrived(cond, u_v.at[s], u_r.at[s])
-        begin(cond, rcopy(u_v.at[s], u_v.at[s], uf_s.at[s], uf_r.at[s], dev(mate, ten)))
+        begin(cond, rcopy(u_v.at[s], u_v.at[s], uf_s.at[0], uf_r.at[0], dev(mate, ten)), sent=True)
+    settle(primary, u_v, uf_s.at[0])
 
     @pl.when(both(lower, primary))
     def _():
@@ -539,8 +597,7 @@
         def _():
             uc_v[j, ten] = um_v[:, cols(j, wcol)]
 
-    for s in range(n_t):
-        arrived(secondary, u_v.at[s], uf_r.at[s])
+    arrived(secondary, u_v, uf_r.at[0])
 
     ub = u_v[...].reshape(rows, width)
     dm = jnp.zeros((rows, wo_v.shape[1]), F32)
@@ -580,69 +637,115 @@
     dcg = dc * lgain
     dl = rl * dcg - l32 * (rl * rl * rl) * jnp.mean(l32 * dcg, axis=1, keepdims=True)
     dlat = jnp.concatenate([dl.astype(BF), drk[:, :ROPE].astype(BF)], axis=1)
+    lp_v[...] = dlat.reshape(n_t, share, dlat.shape[1])
+
+    @pl.when(primary)
+    def _():
+        ls_v[group] = lp_v[ten]
+
+    shared = ((part_v, rs_v), (lp_v, ls_v))
+
+    def share_out(k, gate):
+        source, dest = shared[k]
+        for s in range(n_t):
+            copy = rcopy(source.at[s], dest.at[group], rs_s.at[k], rs_r.at[k], dev(block, s))
+            begin(both(jnp.logical_or(s != ten, secondary), gate), copy, sent=True)
+        settle(both(primary, gate), dest.at[pl.ds(0, n_t - 1)], rs_s.at[k])
+        settle(both(secondary, gate), dest, rs_s.at[k])
+
+    share_out(1, lower)
     dq = query_grad(slopes, heads[0][1], heads[1][1], rk)
     dn = mm_nt(dq, wq) + jnp.concatenate([mm(dlat, wl[d]) for d in range(n)], axis=1)
     part_v[...] = dn.astype(BF).reshape(n_t, share, width)
-    lp_v[...] = dlat.reshape(n_t, share, dlat.shape[1])
-    for k, (source, dest) in enumerate(((part_v, rs_v), (lp_v, ls_v))):
-        for s in range(n_t):
-            begin(
-                jnp.logical_or(s != ten, secondary),
-                rcopy(source.at[s], dest.at[group], rs_s.at[k, s], rs_r.at[k, group], dev(block, s)),
-            )
 
     @pl.when(primary)
     def _():
         rs_v[group] = part_v[ten]
-        ls_v[group] = lp_v[ten]
         sv_v[me] = so_v[...]
 
-    spread_block(1, so_v, sv_v, gate=lower)
-
-    def collect_shares(k, dest):
-        for g in range(n_t):
-            arrived(jnp.logical_or(g != ten, secondary), dest.at[g], rs_r.at[k, g])
-
-    collect_shares(0, rs_v)
-    dns = jnp.sum(rs_v[...].astype(F32), axis=0)
-    dng = dns * gain
-    u_my = um_v[...].astype(F32)
-    dx = u_my + r_my * dng - x_my * (r_my * r_my * r_my) * jnp.mean(x_my * dng, axis=1, keepdims=True)
-    dx_v[...] = dx.astype(BF)
+    share_out(0, last)
+    share_out(1, last)
+    spread_block(3, lower, True)
+    spread_block(3, lower, False)
+    share_out(0, lower)
+
+    def collect_shares(k, gate=True):
+        dest = shared[k][1]
+        arrived(both(primary, gate), dest.at[pl.ds(0, n_t - 1)], rs_r.at[k])
+        arrived(both(secondary, gate), dest, rs_r.at[k])
+
+    def sum_latent(gate):
+        collect_shares(1, gate)
+
+        @pl.when(gate)
+        def _():
+            dl_v[me, ten] = jnp.sum(ls_v[...].astype(F32), axis=0).astype(BF)
+
+        spread_z(3, lambda e: dl_v.at[me, ten], dl_v, me, ten, gate=gate)
+
+    sum_latent(lower)
+    relay(2, uc_v, gate=lower)
+    hand_on(3, lower)
+    relay(3, dl_v, gate=lower)
+    lanes = 128
     below = jnp.maximum(sec - 1, 0)
-    for i in range(n_t // 2):
-        begin(sec > 0, rcopy(dx_v, u_v.at[ten], p_s.at[i], u_r.at[ten], (below, me, 2 * i + par)))
-    begin(both(sec > 0, secondary), rcopy(dx_v, um_v, p_s.at[n_t // 2], um_r.at[0], (below, me, ten)))
-    collect_shares(1, ls_v)
-    dl_v[me, ten] = jnp.sum(ls_v[...].astype(F32), axis=0).astype(BF)
-    spread_z(3, lambda e: dl_v.at[me, ten], dl_v, me, ten)
-    dgain = jnp.sum(dns * x_my * r_my, axis=0, keepdims=True)
-    for j in range(n):
-        piece = jnp.concatenate([dgain[:, cols(j, wcol)], dlg[:, cols(j, ccol)]], axis=1)
-        sg_v[j] = jnp.broadcast_to(piece, sg_v.shape[1:])
-    spread_dp(1, lambda j: sg_v.at[j], sr_v)
-    sr_v[me] = sg_v[me]
-    spread_block(1, so_v, sv_v, gate=last)
-    spread_block(0, fo_v, fw_v, gate=last)
-    for m in range(micros):
-        ig_ref[m] = dx[m * chunk : (m + 1) * chunk].astype(BF)
-    relay(1, cc_v, owned=primary, gate=last)
-    relay(4, rk_v, owned=primary, gate=last)
-    relay(2, uc_v)
-    hand_on(1, sv_v)
-    relay(3, dl_v)
-    hand_on(0, fw_v, gate=last)
-    collect_dp(1, sr_v)
-    st_v[ten] = jnp.sum(sr_v[...], axis=0)
-    for j in range(n_t):
-        begin(j != ten, rcopy(st_v.at[ten], st_v.at[ten], st_s.at[j], st_r.at[ten], dev(me, j)))
-    collect_block(0, fw_v)
-    collect_block(1, sv_v)
+
+    def finish(gate):
+        collect_shares(0, gate)
+
+        @pl.when(gate)
+        def _():
+            dns = jnp.sum(rs_v[...].astype(F32), axis=0)
+            dng = dns * gain
+            u_my = um_v[...].astype(F32)
+            dx = u_my + r_my * dng - x_my * (r_my * r_my * r_my) * jnp.mean(x_my * dng, axis=1, keepdims=True)
+            dx_v[...] = dx.astype(BF)
+
+        for i in range(n_t // 2):
+            copy = rcopy(dx_v, u_v.at[ten], p_s.at[i], u_r.at[ten], (below, me, 2 * i + par))
+            begin(both(sec > 0, gate), copy)
+        copy = rcopy(dx_v, um_v, p_s.at[n_t // 2], um_r.at[0], (below, me, ten))
+        begin(both(both(sec > 0, secondary), gate), copy)
+
+        @pl.when(gate)
+        def _():
+            dgain = jnp.sum(jnp.sum(rs_v[...].astype(F32), axis=0) * x_my * r_my, axis=0, keepdims=True)
+            for j in range(n):
+                piece = jnp.concatenate([dgain[:, cols(j, wcol)], dlg[:, cols(j, ccol)]], axis=1)
+                for i in range(piece.shape[1] // lanes):
+                    sg_v[j, i : i + 1] = piece[:, cols(i, lanes)]
+            sr_v[me * n_t + ten] = sg_v[me]
+            for m in range(micros):
+                ig_ref[m] = dx_v[m * chunk : (m + 1) * chunk]
+
+        for j in range(n):
+            for t in range(n_t):
+                copy = rcopy(sg_v.at[j], sr_v.at[me * n_t + ten], sg_s.at[0], sg_r.at[0], dev(j, t))
+                begin(both(jnp.logical_or(j != me, t != ten), gate), copy, sent=True)
+        settle(gate, sr_v.at[pl.ds(0, n * n_t - 1)], sg_s.at[0])
+
+    finish(lower)
+    finish(last)
+    for across in (True, False):
+        for k in range(4):
+            spread_block(k, last, across)
+    sum_latent(last)
+    relay(0, nc_v, gate=last)
+    relay(1, cc_v, gate=last)
+    relay(4, rk_v, gate=last)
+    relay(2, uc_v, gate=last)
+    for k in range(4):
+        hand_on(k, last)
+    relay(3, dl_v, gate=last)
+    for k in range(4):
+        collect_block(k)
+    for k, dest in ((0, nc_v), (1, cc_v), (2, uc_v), (4, rk_v)):
+        pass_on(k, dest)
     collect(4, rk_v)
     for b in range(n):
         few = sv_v[b, :, :NOPE]
         ds = [jnp.where(same, mm_nt(few, picks[h]), 0.0).astype(BF) for h in range(2)]
-        part = lambda i: fw_v[b, :, cols(i, NOPE)]
+        part = lambda i: fw_v[b, i // 2, :, cols(i % 2, NOPE)]
         dq_v[b] = query_grad(ds, part(2), part(3), rk_v[b].reshape(rows, 2 * ROPE))
         for h in range(2):
             de_v[b, :, cols(2 * h, NOPE)] = mm_tn(ds[h], part(h)).astype(BF)
@@ -652,15 +755,17 @@
     gq_ref[...] = mm_tn(nc_v[...].reshape(n * rows, wcol), dq_v[...].reshape(n * rows, dq_v.shape[2]))
     ge_ref[...] = mm_tn(cc_v[...].reshape(n * rows, ccol), de_v[...].reshape(n * rows, de_v.shape[2]))
     collect(2, uc_v)
-    mixed = fw_v[:, :, 4 * NOPE :].reshape(n * rows, 2 * VDIM)
+    mixed = fw_v[:, 2].reshape(n * rows, 2 * VDIM)
     go_ref[...] = mm_tn(mixed, uc_v[...].reshape(n * rows, wcol))
+    pass_on(3, dl_v)
     collect(3, dl_v)
     gl_ref[...] = mm_tn(dl_v[...].reshape(n * rows, dl_v.shape[3]), nc_v[...].reshape(n * rows, wcol))
-    for j in range(n_t):
-        arrived(j != ten, st_v.at[j], st_r.at[j])
-    summed = jnp.sum(st_v[...], axis=0)
-    gg_ref[...] = summed[0:1, :wcol]
-    glg_ref[...] = summed[0:1, wcol:]
+    arrived(me >= 0, sr_v.at[pl.ds(0, n * n_t - 1)], sg_r.at[0])
+    summed = jnp.sum(sr_v[...], axis=0)
+    for i in range(wcol // lanes):
+        gg_ref[:, cols(i, lanes)] = summed[i : i + 1]
+    for i in range(ccol // lanes):
+        glg_ref[:, cols(i, lanes)] = summed[wcol // lanes + i : wcol // lanes + i + 1]
     for cond, copy in drains:
         @pl.when(cond)
         def _(copy=copy):
@@ -724,8 +829,8 @@
             pltpu.VMEM((n, n_t, share, lcols), BF),
             pltpu.VMEM((n, n_t, share, 2 * ROPE), BF),
             pltpu.VMEM((rows, 2 * ROPE), BF),
-            pltpu.VMEM((rows, 4 * NOPE + orows), BF),
-            pltpu.VMEM((n, rows, 4 * NOPE + orows), BF),
+            pltpu.VMEM((3, rows, orows), BF),
+            pltpu.VMEM((n, 3, rows, orows), BF),
             pltpu.VMEM((rows, NOPE + orows), BF),
             pltpu.VMEM((n, rows, NOPE + orows), BF),
             pltpu.VMEM((n_t, share, width), BF),
@@ -733,15 +838,14 @@
             pltpu.VMEM((n_t, share, lcols), BF),
             pltpu.VMEM((n_t, share, lcols), BF),
             pltpu.VMEM((share, width), BF),
-            pltpu.VMEM((n, 8, small), F32),
-            pltpu.VMEM((n, 8, small), F32),
-            pltpu.VMEM((n_t, 8, small), F32),
+            pltpu.VMEM((n, 8 * -(-small // 1024), 128), F32),
+            pltpu.VMEM((n * n_t, 8 * -(-small // 1024), 128), F32),
             pltpu.VMEM((n, rows, qcols), BF),
             pltpu.VMEM((n, rows, ecols), BF),
-            sem(2, n), sem(2, n), sem(1), sem(1), sem(2), sem(n), sem(n), sem(n, n_t), sem(n, n_t),
-            sem(3, n // 2), sem(3, n), sem(3, n), sem(3, n), sem(5, n), sem(5, n), sem(5, n, n_t), sem(5, n, n_t),
-            sem(2, n), sem(2, n), sem(2, n), sem(2, n_t), sem(2, n_t), sem(n_t // 2 + 1), sem(n_t), sem(1), sem(n_t), sem(n_t),
-            sem(n_t), sem(n_t),
+            sem(1), sem(1), sem(1), sem(1), sem(1), sem(n), sem(1), sem(1), sem(1),
+            sem(3), sem(3, n), sem(3), sem(3), sem(5), sem(5), sem(n), sem(5), sem(5), sem(5),
+            sem(4), sem(4, n), sem(4), sem(2), sem(2), sem(n_t // 2 + 1), sem(n_t), sem(1), sem(1), sem(1),
+            sem(1), sem(1),
         ],
         compiler_params=pltpu.CompilerParams(
             collective_id=0, has_side_effects=True, vmem_limit_bytes=60 * 1024 * 1024

time: 84.5 us -> 77.3 us (0.915)
  Pallas kernels: 82.3 us -> 75.3 us
    pallas_call x1, Pallas kernels: 81.1 us -> 74 us  [section_step(): pl.pallas_call(lambda *refs: section_kernel((n_pipe, n, n_t, micros, seq)...]
where the time goes in v3:
time: 77.3 us; the launch traced here: 75.9 us
  Pallas kernels  75.3 us (97%)
    pallas_call x1, Pallas kernels, section_step(): pl.pallas_call(lambda *refs: section_kernel((n_pipe, n, n_t, micros, seq)...  74 us

profile of v3, /device:TPU:0, one launch (start us, length us, event | category | flops | bytes accessed | tf_op | source)
XLA Modules:
  0.0 75.9 jit_solution(5111260332005535261)
XLA Ops:
  0.6 74.0 %section_step.1 = (bf16[2,16,1024]{2,1,0:T(8,128)(2,1)S(1)}, f32[1,256]{1,0:T(1,128)S(1)}, f32[256,384]{1,0:T(8,128)S(1)}, f32[576,256]{1,0:T(8,128)S(1)}, f32[1...) custom-call(bf16[2,64,1024]{2,1,0:T(8,128)(2,1)} %bitcast.15, bf16[2,64,1024]{2,1,0:T(8,128)(2,1)} %refs_1_.1, ...), custom_call_target="tpu_custom_call" | custom-call | tf_op jit(solution)/shard_map/section_step/pallas_call | solution.py:799
  74.7 1.2 %hand_over.1 = (bf16[2,16,1024]{2,1,0:T(8,128)(2,1)}, f32[1,256]{1,0:T(1,128)}, f32[256,384]{1,0:T(8,128)}, f32[576,256]{1,0:T(8,128)}, f32[1,128]{1,0:T(1,128)}...) custom-call(bf16[2,16,1024]{2,1,0:T(8,128)(2,1)S(1)} %get-tuple-element.21.refs_0_, f32[1,256]{1,0:T(1,128)S(1)} %get-tuple-element.22.refs_1_, ...), custom_call_target="tpu_custom_call" | custom-call | tf_op jit(solution)/shard_map/hand_over/pallas_call | solution.py:858

commit v4 on v3

--- a/solution.py
+++ b/solution.py
@@ -214,13 +214,14 @@
 
 def section_kernel(
     dims,
+    saved_in, top_in, gain_in, lgain_in, wq_in, wl_in, we_in, wo_in, cos_in, sin_in,
+    ig_ref, gg_ref, gq_ref, gl_ref, glg_ref, ge_ref, go_ref,
     saved_ref, top_ref, gain_ref, lgain_ref, wq_ref, wl_ref, we_ref, wo_ref, cos_ref, sin_ref,
-    ig_ref, gg_ref, gq_ref, gl_ref, glg_ref, ge_ref, go_ref,
     x_v, xs_v, own_v, sm_v, nm_v, u_v, um_v, cb_v, wq_v, wl_v, we_v, wo_v,
     nc_v, cc_v, uc_v, dl_v, rk_v, ro_v, fo_v, fw_v, so_v, sv_v, part_v, rs_v, lp_v, ls_v, dx_v, sg_v, sr_v,
     dq_v, de_v,
     dp_s, dp_r, x_s, x_r, wz_s, wz_r, wh_s, wt_s, wt_r, w_s, w_r, f_s, f_r, z_s, z_r, zl_r, t_s, ta_r, tb_r,
-    b_s, b_r, bh_s, rs_s, rs_r, p_s, u_r, um_r, uf_s, uf_r, sg_s, sg_r,
+    b_s, b_r, bh_s, rs_s, rs_r, p_s, u_r, um_r, uf_s, uf_r, sg_s, sg_r, in_s,
 ):
     n_pipe, n, n_t, micros, seq = dims
     sec, me, ten = lax.axis_index("pipe"), lax.axis_index("dp"), lax.axis_index("tensor")
@@ -290,16 +291,11 @@
     def u_store(j, m, value):
         u_v[j, m * chunk : (m + 1) * chunk] = value
 
-    own_v[:, :wcol] = jnp.broadcast_to(gain_ref[...].astype(F32), (8, wcol))
-    own_v[:, wcol:] = jnp.broadcast_to(lgain_ref[...].astype(F32), (8, ccol))
-
-    @pl.when(last)
-    def _():
-        um_v[...] = mine(top_ref)
-
-    @pl.when(both(last, primary))
-    def _():
-        by_share(u_store, top_ref)
+    inputs = (saved_in, top_in, gain_in, lgain_in, wq_in, wl_in, we_in, wo_in, cos_in, sin_in)
+    places = (saved_ref, top_ref, gain_ref, lgain_ref, wq_ref, wl_ref, we_ref, wo_ref, cos_ref, sin_ref)
+    fetches = [pltpu.make_async_copy(a, b, in_s.at[i]) for i, (a, b) in enumerate(zip(inputs, places))]
+    for copy in fetches:
+        copy.start()
 
     barrier = pltpu.get_barrier_semaphore()
     for j in range(n_t):
@@ -315,6 +311,20 @@
         @pl.when(lower)
         def _():
             pl.semaphore_signal(barrier, inc=1, device_id=(sec + 1, me, j), device_id_type=MESH)
+
+    for copy in fetches:
+        copy.wait()
+
+    own_v[:, :wcol] = jnp.broadcast_to(gain_ref[...].astype(F32), (8, wcol))
+    own_v[:, wcol:] = jnp.broadcast_to(lgain_ref[...].astype(F32), (8, ccol))
+
+    @pl.when(last)
+    def _():
+        um_v[...] = mine(top_ref)
+
+    @pl.when(both(last, primary))
+    def _():
+        by_share(u_store, top_ref)
 
     neighbours = jnp.minimum(sec, 1) + jnp.minimum(n_pipe - 1 - sec, 1)
     pl.semaphore_wait(barrier, n * n_t - 1 + neighbours * n_t)
@@ -361,12 +371,13 @@
             for b in range(n):
                 share_slot(b)
 
-    def pass_on(k, dest):
-        arrived(me >= 0, dest.at[pl.ds(0, n), opposite], ta_r.at[k])
+    def pass_on(k, dest, gate=True):
+        gate = both(me >= 0, gate)
+        arrived(gate, dest.at[pl.ds(0, n), opposite], ta_r.at[k])
         for b in range(n):
             at = dest.at[b, opposite]
-            begin(me >= 0, rcopy(at, at, t_s.at[k], tb_r.at[k], dev(me, partner)), sent=True)
-        settle(me >= 0, dest.at[pl.ds(0, n - 1)], t_s.at[k])
+            begin(gate, rcopy(at, at, t_s.at[k], tb_r.at[k], dev(me, partner)), sent=True)
+        settle(gate, dest.at[pl.ds(0, n - 1)], t_s.at[k])
 
     def collect(k, dest):
         arrived(me >= 0, dest.at[pl.ds(0, 2)], tb_r.at[k])
@@ -647,7 +658,8 @@
 
     def share_out(k, gate):
         source, dest = shared[k]
-        for s in range(n_t):
+        for i in range(n_t):
+            s = lax.rem(ten - core + 2 + i, n_t)
             copy = rcopy(source.at[s], dest.at[group], rs_s.at[k], rs_r.at[k], dev(block, s))
             begin(both(jnp.logical_or(s != ten, secondary), gate), copy, sent=True)
         settle(both(primary, gate), dest.at[pl.ds(0, n_t - 1)], rs_s.at[k])
@@ -665,8 +677,8 @@
 
     share_out(0, last)
     share_out(1, last)
+    spread_block(3, lower, False)
     spread_block(3, lower, True)
-    spread_block(3, lower, False)
     share_out(0, lower)
 
     def collect_shares(k, gate=True):
@@ -683,6 +695,8 @@
 
         spread_z(3, lambda e: dl_v.at[me, ten], dl_v, me, ten, gate=gate)
 
+    for k, dest in ((0, nc_v), (1, cc_v), (4, rk_v)):
+        pass_on(k, dest, lower)
     sum_latent(lower)
     relay(2, uc_v, gate=lower)
     hand_on(3, lower)
@@ -702,7 +716,8 @@
             dx_v[...] = dx.astype(BF)
 
         for i in range(n_t // 2):
-            copy = rcopy(dx_v, u_v.at[ten], p_s.at[i], u_r.at[ten], (below, me, 2 * i + par))
+            to = lax.rem(ten - core + 2 + 2 * i, n_t) + par
+            copy = rcopy(dx_v, u_v.at[ten], p_s.at[i], u_r.at[ten], (below, me, to))
             begin(both(sec > 0, gate), copy)
         copy = rcopy(dx_v, um_v, p_s.at[n_t // 2], um_r.at[0], (below, me, ten))
         begin(both(both(sec > 0, secondary), gate), copy)
@@ -734,13 +749,14 @@
     relay(1, cc_v, gate=last)
     relay(4, rk_v, gate=last)
     relay(2, uc_v, gate=last)
+    for k, dest in ((0, nc_v), (1, cc_v), (4, rk_v)):
+        pass_on(k, dest, last)
     for k in range(4):
         hand_on(k, last)
     relay(3, dl_v, gate=last)
     for k in range(4):
         collect_block(k)
-    for k, dest in ((0, nc_v), (1, cc_v), (2, uc_v), (4, rk_v)):
-        pass_on(k, dest)
+    pass_on(2, uc_v)
     collect(4, rk_v)
     for b in range(n):
         few = sv_v[b, :, :NOPE]
@@ -791,6 +807,10 @@
     sign = np.where(np.arange(2 * ROPE) % ROPE < ROPE // 2, -1.0, 1.0)
     cosine = jnp.asarray(np.cos(angle), F32)
     sine = jnp.asarray(np.sin(angle) * sign, F32)
+    operands = (
+        saved[0], top_grad, gain, compressed_gain, w_query[0], w_latent[0].T,
+        expand_weight[0], w_output[0], cosine, sine,
+    )
     vm = pl.BlockSpec(memory_space=pltpu.VMEM)
     shape = jax.ShapeDtypeStruct
     kept = pltpu.VMEM
@@ -808,9 +828,10 @@
             kept((ccol, ecols), F32),
             kept((orows, wcol), F32),
         ),
-        in_specs=[vm] * 10,
+        in_specs=[pl.BlockSpec(memory_space=pl.ANY)] * 10,
         out_specs=(vm,) * 7,
         scratch_shapes=[
+            *(pltpu.VMEM(a.shape, a.dtype) for a in operands),
             pltpu.VMEM((rows, width), BF),
             pltpu.VMEM((micros, seq, width), BF),
             pltpu.VMEM((8, small), F32),
@@ -845,15 +866,12 @@
             sem(1), sem(1), sem(1), sem(1), sem(1), sem(n), sem(1), sem(1), sem(1),
             sem(3), sem(3, n), sem(3), sem(3), sem(5), sem(5), sem(n), sem(5), sem(5), sem(5),
             sem(4), sem(4, n), sem(4), sem(2), sem(2), sem(n_t // 2 + 1), sem(n_t), sem(1), sem(1), sem(1),
-            sem(1), sem(1),
+            sem(1), sem(1), sem(len(operands)),
         ],
         compiler_params=pltpu.CompilerParams(
             collective_id=0, has_side_effects=True, vmem_limit_bytes=60 * 1024 * 1024
         ),
-    )(
-        saved[0], top_grad, gain, compressed_gain, w_query[0], w_latent[0].T,
-        expand_weight[0], w_output[0], cosine, sine,
-    )
+    )(*operands)
     parts = [pltpu.with_memory_space_constraint(p, pltpu.VMEM) for p in (ig, gg, gq, gl, glg, ge, go)]
     ig, gg, gq, gl, glg, ge, go = pl.pallas_call(
         hand_over,

time: 77.3 us -> 75.2 us (0.973); the launches traced: 75.9 us -> 74.8 us
  Pallas kernels: 75.3 us -> 74.1 us
    pallas_call x1, Pallas kernels: 74 us -> 72.9 us  [section_step(): pl.pallas_call(lambda *refs: section_kernel((n_pipe, n, n_t, micros, seq)...]
where the time goes in v4:
time: 75.2 us; the launch traced here: 74.8 us
  Pallas kernels  74.1 us (99%)
    pallas_call x1, Pallas kernels, section_step(): pl.pallas_call(lambda *refs: section_kernel((n_pipe, n, n_t, micros, seq)...  72.9 us

profile of v4, /device:TPU:0, one launch (start us, length us, event | category | flops | bytes accessed | tf_op | source)
XLA Modules:
  0.0 74.8 jit_solution(11706331810073486957)
XLA Ops:
  0.6 72.9 %section_step.1 = (bf16[2,16,1024]{2,1,0:T(8,128)(2,1)S(1)}, f32[1,256]{1,0:T(1,128)S(1)}, f32[256,384]{1,0:T(8,128)S(1)}, f32[576,256]{1,0:T(8,128)S(1)}, f32[1...) custom-call(bf16[2,64,1024]{2,1,0:T(8,128)(2,1)} %bitcast.15, bf16[2,64,1024]{2,1,0:T(8,128)(2,1)} %refs_1_.1, ...), custom_call_target="tpu_custom_call" | custom-call | tf_op jit(solution)/shard_map/section_step/pallas_call | solution.py:819
  73.5 1.2 %hand_over.1 = (bf16[2,16,1024]{2,1,0:T(8,128)(2,1)}, f32[1,256]{1,0:T(1,128)}, f32[256,384]{1,0:T(8,128)}, f32[576,256]{1,0:T(8,128)}, f32[1,128]{1,0:T(1,128)}...) custom-call(bf16[2,16,1024]{2,1,0:T(8,128)(2,1)S(1)} %get-tuple-element.21.refs_0_, f32[1,256]{1,0:T(1,128)S(1)} %get-tuple-element.22.refs_1_, ...), custom_call_target="tpu_custom_call" | custom-call | tf_op jit(solution)/shard_map/hand_over/pallas_call | solution.py:876

commit v5 on v4

--- a/solution.py
+++ b/solution.py
@@ -396,14 +396,17 @@
             settle(both(gate, primary), several(2), b_s.at[k])
             settle(both(gate, secondary), several(3), b_s.at[k])
 
-    def hand_on(k, gate):
+    def hand_on(k, gate, early=None):
         for b in range(n):
             cond = both(both(middle, half != b // 2), gate)
+            if early is not None:
+                cond = both(cond, core == b % 2 if early else core != b % 2)
             at = landing(k, b)
             arrived(cond, at, b_r.at[k, b])
             begin(cond, rcopy(at, at, bh_s.at[k], b_r.at[k, b], dev(mate, ten)), sent=True)
         two = sv_v.at[pl.ds(0, 2)] if k == 3 else fw_v.at[pl.ds(0, 2), k]
-        settle(both(middle, gate), two, bh_s.at[k])
+        if not early:
+            settle(both(middle, gate), two, bh_s.at[k])
 
     def collect_block(k):
         for b in range(n):
@@ -679,7 +682,6 @@
     share_out(1, last)
     spread_block(3, lower, False)
     spread_block(3, lower, True)
-    share_out(0, lower)
 
     def collect_shares(k, gate=True):
         dest = shared[k][1]
@@ -697,9 +699,11 @@
 
     for k, dest in ((0, nc_v), (1, cc_v), (4, rk_v)):
         pass_on(k, dest, lower)
+    hand_on(3, lower, early=True)
     sum_latent(lower)
+    share_out(0, lower)
     relay(2, uc_v, gate=lower)
-    hand_on(3, lower)
+    hand_on(3, lower, early=False)
     relay(3, dl_v, gate=lower)
     lanes = 128
     below = jnp.maximum(sec - 1, 0)
@@ -766,6 +770,7 @@
         for h in range(2):
             de_v[b, :, cols(2 * h, NOPE)] = mm_tn(ds[h], part(h)).astype(BF)
             de_v[b, :, cols(2 * h + 1, NOPE)] = sv_v[b, :, cols(1 + h, VDIM)]
+    pass_on(3, dl_v)
     collect(0, nc_v)
     collect(1, cc_v)
     gq_ref[...] = mm_tn(nc_v[...].reshape(n * rows, wcol), dq_v[...].reshape(n * rows, dq_v.shape[2]))
@@ -773,7 +778,6 @@
     collect(2, uc_v)
     mixed = fw_v[:, 2].reshape(n * rows, 2 * VDIM)
     go_ref[...] = mm_tn(mixed, uc_v[...].reshape(n * rows, wcol))
-    pass_on(3, dl_v)
     collect(3, dl_v)
     gl_ref[...] = mm_tn(dl_v[...].reshape(n * rows, dl_v.shape[3]), nc_v[...].reshape(n * rows, wcol))
     arrived(me >= 0, sr_v.at[pl.ds(0, n * n_t - 1)], sg_r.at[0])

time: 75.2 us -> 74.7 us (level)
  no operation moved by 1% of the time
where the time goes in v5:
time: 74.7 us; the launch traced here: 74.6 us
  Pallas kernels  73.9 us (99%)
    pallas_call x1, Pallas kernels, section_step(): pl.pallas_call(lambda *refs: section_kernel((n_pipe, n, n_t, micros, seq)...  72.7 us

profile of v5, /device:TPU:0, one launch (start us, length us, event | category | flops | bytes accessed | tf_op | source)
XLA Modules:
  0.0 74.6 jit_solution(8572157738039190617)
XLA Ops:
  0.6 72.7 %section_step.1 = (bf16[2,16,1024]{2,1,0:T(8,128)(2,1)S(1)}, f32[1,256]{1,0:T(1,128)S(1)}, f32[256,384]{1,0:T(8,128)S(1)}, f32[576,256]{1,0:T(8,128)S(1)}, f32[1...) custom-call(bf16[2,64,1024]{2,1,0:T(8,128)(2,1)} %bitcast.15, bf16[2,64,1024]{2,1,0:T(8,128)(2,1)} %refs_1_.1, ...), custom_call_target="tpu_custom_call" | custom-call | tf_op jit(solution)/shard_map/section_step/pallas_call | solution.py:823
  73.3 1.2 %hand_over.1 = (bf16[2,16,1024]{2,1,0:T(8,128)(2,1)}, f32[1,256]{1,0:T(1,128)}, f32[256,384]{1,0:T(8,128)}, f32[576,256]{1,0:T(8,128)}, f32[1,128]{1,0:T(1,128)}...) custom-call(bf16[2,16,1024]{2,1,0:T(8,128)(2,1)S(1)} %get-tuple-element.21.refs_0_, f32[1,256]{1,0:T(1,128)S(1)} %get-tuple-element.22.refs_1_, ...), custom_call_target="tpu_custom_call" | custom-call | tf_op jit(solution)/shard_map/hand_over/pallas_call | solution.py:880

commit v6 on v5

--- a/solution.py
+++ b/solution.py
@@ -793,8 +793,11 @@
 
 
 def hand_over(*refs):
-    for source, dest in zip(refs[:7], refs[7:]):
-        dest[...] = source[...]
+    copies = [pltpu.make_async_copy(refs[i], refs[7 + i], refs[14].at[i]) for i in range(7)]
+    for copy in copies:
+        copy.start()
+    for copy in copies:
+        copy.wait()
 
 
 def section_step(saved, top_grad, gain, w_query, w_latent, compressed_gain, expand_weight, w_output):
@@ -882,7 +885,8 @@
         name="hand_over",
         out_shape=tuple(shape(p.shape, p.dtype) for p in parts),
         in_specs=[vm] * 7,
-        out_specs=(vm,) * 7,
+        out_specs=(pl.BlockSpec(memory_space=pl.ANY),) * 7,
+        scratch_shapes=[sem(7)],
     )(*parts)
     return ig[None], gg, gq[None], gl.T[None], glg, ge[None], go[None]
 

time: 74.7 us -> 74.7 us (level)
  no operation moved by 1% of the time
where the time goes in v6:
time: 74.7 us; the launch traced here: 74.5 us
  Pallas kernels  73.9 us (99%)
    pallas_call x1, Pallas kernels, section_step(): pl.pallas_call(lambda *refs: section_kernel((n_pipe, n, n_t, micros, seq)...  72.7 us

profile of v6, /device:TPU:0, one launch (start us, length us, event | category | flops | bytes accessed | tf_op | source)
XLA Modules:
  0.0 74.5 jit_solution(12535869129934984314)
XLA Ops:
  0.6 72.7 %section_step.1 = (bf16[2,16,1024]{2,1,0:T(8,128)(2,1)S(1)}, f32[1,256]{1,0:T(1,128)S(1)}, f32[256,384]{1,0:T(8,128)S(1)}, f32[576,256]{1,0:T(8,128)S(1)}, f32[1...) custom-call(bf16[2,64,1024]{2,1,0:T(8,128)(2,1)} %bitcast.15, bf16[2,64,1024]{2,1,0:T(8,128)(2,1)} %refs_1_.1, ...), custom_call_target="tpu_custom_call" | custom-call | tf_op jit(solution)/shard_map/section_step/pallas_call | solution.py:826
  73.3 1.2 %hand_over.1 = (bf16[2,16,1024]{2,1,0:T(8,128)(2,1)}, f32[1,256]{1,0:T(1,128)}, f32[256,384]{1,0:T(8,128)}, f32[576,256]{1,0:T(8,128)}, f32[1,128]{1,0:T(1,128)}...) custom-call(bf16[2,16,1024]{2,1,0:T(8,128)(2,1)S(1)} %get-tuple-element.21.refs_0_, f32[1,256]{1,0:T(1,128)S(1)} %get-tuple-element.22.refs_1_, ...), custom_call_target="tpu_custom_call" | custom-call | tf_op jit(solution)/shard_map/hand_over/pallas_call | solution.py:883
